TPU v7x, 128 devices: a whole 4x4x4 slice. The times are simulated.
128 devices in a mesh: point: 32 (over z_hi, x, y), batch: 4 (over z_lo, core).
Axes of the slice: x: 4, y: 4, z: 4 (z_hi: 2, z_lo: 2; z = z_hi * 2 + z_lo), core: 2. Of those that a mesh axis runs over, the one named last changes fastest.
Arguments:
- activations: bfloat16 [128, 14, 14, 1024], P('batch'), may hold values from -8 to 8
- labels: int32 [128], P('batch'), may hold values from 0 to 999
- t_values: float32 [64], replicated, may hold values from 0 to 1
- point_index: int32 [32], replicated, may hold values from 0 to 63
- w_reduce: bfloat16 [3, 1024, 256], P(None, 'point'), may hold values from -1 to 1
- w_spatial: bfloat16 [3, 2304, 256], P(None, 'point'), may hold values from -0.125 to 0.125
- w_expand: bfloat16 [3, 256, 1024], P(None, 'point'), may hold values from -0.375 to 0.375
- w_classes: bfloat16 [3, 1000, 1024], P(None, None, 'point'), may hold values from -0.1875 to 0.1875
- norm_gain: float32 [3, 1536], replicated, may hold values from 0.5 to 1.5
- norm_bias: float32 [3, 1536], replicated, may hold values from -3 to 3
- class_bias: float32 [3, 1000], replicated, may hold values from -3 to 3
Outputs:
- mean_reduce: float32 [32, 256], P('point')
- var_reduce: float32 [32, 256], P('point')
- mean_spatial: float32 [32, 256], P('point')
- var_spatial: float32 [32, 256], P('point')
- mean_expand: float32 [32, 1024], P('point')
- var_expand: float32 [32, 1024], P('point')
- margin: float32 [32], replicated
All inputs are finite; a program needn't handle non-finite values.
Results may differ from a plain program's by a relative error of at most 0.003.
Values may be sent and summed in bfloat16 or wider, within the bound.
No kernel may reach another device: no remote copies, remote signals or barrier semaphores. Data moves between devices by JAX's collectives and lax.ppermute only.
A program may use at most 128 MiB of HBM per device.

v0:
```python
import jax
import jax.numpy as jnp
from jax import lax
from jax.sharding import Mesh
from jax.sharding import PartitionSpec as P

BATCH = ("batch_0", "batch_1")


EPSILON = 1e-05


def by_axis(x, axes):
    for axis in axes:
        x = lax.psum(x, axis)
    return x


def sent_to_all(x, axis):
    copies = jnp.broadcast_to(x, (lax.axis_size(axis), *x.shape))
    return lax.all_to_all(copies, axis, split_axis=0, concat_axis=0, tiled=True)


def over_copies(x, axis):
    everything = sent_to_all(x, axis)
    return jnp.sum(everything, axis=0)


def joined_along(blocks, dim):
    blocks = jnp.moveaxis(blocks, 0, dim)
    dims = blocks.shape
    return blocks.reshape(*dims[:dim], dims[dim] * dims[dim + 1], *dims[dim + 2 :])


def gather_directly(x, axis, dim):
    blocks = sent_to_all(x, axis)
    return joined_along(blocks, dim)


def curve_coefficients(t_values, point_index):
    table_size = t_values.shape[0]
    matches = point_index[:, None] == jnp.arange(table_size, dtype=jnp.int32)[None, :]
    picked = jnp.sum(jnp.where(matches, t_values[None, :], 0.0), axis=1)
    doubled = 2.0 * picked
    return jnp.stack(
        [
            jnp.maximum(1.0 - doubled, 0.0),
            1.0 - jnp.abs(1.0 - doubled),
            jnp.maximum(doubled - 1.0, 0.0),
        ],
        axis=1,
    )


def blend_all(coefficients, endpoints):
    target_shape = (coefficients.shape[0],) + (1,) * (endpoints.ndim - 1)
    start_part = coefficients[:, 0].reshape(target_shape) * endpoints[0].astype(jnp.float32)[None]
    bend_part = coefficients[:, 1].reshape(target_shape) * endpoints[1].astype(jnp.float32)[None]
    final_part = coefficients[:, 2].reshape(target_shape) * endpoints[2].astype(jnp.float32)[None]
    return start_part + bend_part + final_part


def point_weight(endpoints, coefficients, by_columns):
    all_points = blend_all(coefficients, endpoints).astype(jnp.bfloat16)
    if by_columns:
        received = lax.all_to_all(all_points, "point", split_axis=0, concat_axis=2, tiled=True)
    else:
        received = lax.all_to_all(all_points, "point", split_axis=0, concat_axis=1, tiled=True)
    return received[0]


def map_product(maps, kernel):
    return lax.dot_general(
        maps, kernel, (((3,), (0,)), ((), ())), preferred_element_type=jnp.float32
    )


def batch_norm(pre_norm, gain_part, bias_part, row_count):
    channel_total, channel_squares = (
        by_axis(jnp.sum(pre_norm, axis=(0, 1, 2)), BATCH),
        by_axis(jnp.sum(pre_norm * pre_norm, axis=(0, 1, 2)), BATCH),
    )
    channel_mean = channel_total / row_count
    channel_var = channel_squares / row_count - channel_mean * channel_mean
    scaled = (pre_norm - channel_mean) * lax.rsqrt(channel_var + EPSILON) * gain_part + bias_part
    return (channel_mean, channel_var, scaled)


def spatial_conv(source, kernel):
    side_len = source.shape[1]
    middle = source.shape[3]
    padded = jnp.pad(source, ((0, 0), (1, 1), (1, 1), (0, 0)))
    widened = jnp.concatenate(
        [
            padded[:, :, 0:side_len, :],
            padded[:, :, 1 : side_len + 1, :],
            padded[:, :, 2 : side_len + 2, :],
        ],
        axis=3,
    )
    summed = map_product(widened[:, 0:side_len], kernel[0 : 3 * middle])
    summed = summed + map_product(widened[:, 1 : side_len + 1], kernel[3 * middle : 6 * middle])
    summed = summed + map_product(widened[:, 2 : side_len + 2], kernel[6 * middle : 9 * middle])
    return summed


def shards(
    activations,
    labels,
    t_values,
    point_index,
    w_reduce,
    w_spatial,
    w_expand,
    w_classes,
    norm_gain,
    norm_bias,
    class_bias,
):
    coefficients = curve_coefficients(t_values, point_index)
    own_row = lax.dynamic_slice_in_dim(coefficients, lax.axis_index("point"), 1, 0)
    reduce_w = point_weight(w_reduce, coefficients, False)
    spatial_w = point_weight(w_spatial, coefficients, False)
    expand_w = point_weight(w_expand, coefficients, False)
    class_w = point_weight(w_classes, coefficients, True)
    gain_now = blend_all(own_row, norm_gain)[0]
    bias_now = blend_all(own_row, norm_bias)[0]
    shift_now = blend_all(own_row, class_bias)[0]
    images, side_len, _, channels = activations.shape
    middle = w_reduce.shape[2]
    row_count = float(images * side_len * side_len * lax.axis_size(BATCH))
    reduced = map_product(activations, reduce_w)
    mean_one, var_one, normed_one = batch_norm(
        reduced, gain_now[:middle], bias_now[:middle], row_count
    )
    first = jax.nn.relu(normed_one).astype(jnp.bfloat16)
    spatial = spatial_conv(first, spatial_w)
    mean_two, var_two, normed_two = batch_norm(
        spatial, gain_now[middle : 2 * middle], bias_now[middle : 2 * middle], row_count
    )
    second = jax.nn.relu(normed_two).astype(jnp.bfloat16)
    expanded = map_product(second, expand_w)
    mean_three, var_three, normed_three = batch_norm(
        expanded, gain_now[2 * middle :], bias_now[2 * middle :], row_count
    )
    block_out = jax.nn.relu(normed_three + activations.astype(jnp.float32))
    pooled = jnp.mean(block_out, axis=(1, 2)).astype(jnp.bfloat16)
    logits = (
        lax.dot_general(
            pooled, class_w, (((1,), (1,)), ((), ())), preferred_element_type=jnp.float32
        )
        + shift_now
    )
    classes = logits.shape[1]
    onehot = labels[:, None] == jnp.arange(classes, dtype=jnp.int32)[None, :]
    correct = jnp.sum(jnp.where(onehot, logits, 0.0), axis=1)
    rivals = jnp.max(jnp.where(onehot, -1e30, logits), axis=1)
    partial_value = jnp.sum(correct - rivals) / (images * lax.axis_size(BATCH))
    group_sum = over_copies(partial_value.reshape(1), BATCH)
    margin_all = gather_directly(group_sum, "point", 0)
    return (
        mean_one[None],
        var_one[None],
        mean_two[None],
        var_two[None],
        mean_three[None],
        var_three[None],
        margin_all,
    )


def solution(mesh):
    torus = Mesh(mesh.devices.reshape(mesh.shape["point"], 2, 2), ("point", "batch_0", "batch_1"))
    return jax.shard_map(
        shards,
        mesh=torus,
        in_specs=(
            P(BATCH, None, None, None),
            P(BATCH),
            P(),
            P(),
            P(None, "point", None),
            P(None, "point", None),
            P(None, "point", None),
            P(None, None, "point"),
            P(),
            P(),
            P(),
        ),
        out_specs=(
            P("point", None),
            P("point", None),
            P("point", None),
            P("point", None),
            P("point", None),
            P("point", None),
            P(),
        ),
        check_vma=False,
    )
```

profile of v0, /device:TPU:0, one launch (start us, length us, event | category | flops | bytes accessed | tf_op | source)
XLA Modules:
  0.0 189.2 jit_solution(16724359364042612514)
XLA Ops:
  0.6 0.8 bitcast_convert_fusion.11
  1.4 0.8 select_reduce_fusion.2
  2.3 1.1 add_convert_fusion.3
  3.3 10.7 %all-to-all-start = ((bf16[32,32,256]{2,1,0:T(8,128)(2,1)}), bf16[32,32,256]{2,1,0:T(8,128)(2,1)S(1)}, u32[]{:S(2)}, u32[]{:S(2)}) async-start(bf16[32,32,256]{2,1,0:T(8,128)(2,1)} %add_convert_fusion.3), calls=%async_computation | async-start | bytes 1048576 | tf_op jit(solution)/shard_map/all_to_all | solution.py:68
  14.1 0.1 constant_dynamic-slice_fusion
  14.2 0.5 fusion.17
  14.7 2.8 %multiply_add_fusion = (f32[1,1536]{1,0:T(1,128)S(1)}, f32[1,1536]{1,0:T(1,128)S(1)}) fusion(f32[3,1536]{1,0:T(4,128)} %param.20, f32[]{:T(128)} %bitcast.13, f32[]{:T(128)} %bitcast.12, f32[]{:T(128)} %bitcast.11, f32[3,1536]{1,0:T(4,128)} %param.19), kind=kLoop, calls=%fused_computation.48 | loop fusion | flops 15360 | bytes 49164 | tf_op jit(solution)/shard_map/add | solution.py:60
  17.6 0.8 bitcast_convert_fusion.5
  18.4 0.8 bitcast_convert_fusion.8
  19.1 2.8 %multiply_add_fusion.2 = f32[1,1000]{1,0:T(1,128)S(1)} fusion(f32[3,1000]{1,0:T(4,128)} %param.21, f32[]{:T(128)} %bitcast.13, f32[]{:T(128)} %bitcast.12, f32[]{:T(128)} %bitcast.11), kind=kLoop, calls=%fused_computation.50 | loop fusion | flops 5000 | bytes 16012 | tf_op jit(solution)/shard_map/add | solution.py:60
  21.9 0.9 bitcast_convert_fusion.2
  22.9 1.6 add_convert_fusion.1
  24.5 1.1 add_convert_fusion.2
  25.6 2.4 %add_convert_fusion = bf16[32,1000,32]{1,2,0:T(8,128)(2,1)} fusion(f32[1000,32]{0,1:T(8,128)S(1)} %get-tuple-element.37, f32[32]{0:T(128)S(1)} %get-tuple-element.60, f32[1000,32]{0,1:T(8,128)S(1)} %get-tuple-element.38, f32[32]{0:T(128)S(1)} %get-tuple-element.61, f32[1000,32]{0,1:T(8,128)S(1)} %get-tuple-element.36, f32[32]{0:T(128)S(1)} %get-tuple-element.62), kind=kLoop, calls=%fused_computation.8 | loop fusion | flops 6144000 | bytes 2432384 | tf_op jit(solution)/shard_map/convert_element_type | solution.py:64
  27.9 0.0 all-to-all-done
  27.9 9.8 %all-to-all-start.1 = ((bf16[32,72,256]{2,1,0:T(8,128)(2,1)}), bf16[32,72,256]{2,1,0:T(8,128)(2,1)S(1)}, u32[]{:S(2)}, u32[]{:S(2)}) async-start(bf16[32,72,256]{2,1,0:T(8,128)(2,1)} %add_convert_fusion.1), calls=%async_computation.1 | async-start | bytes 2359296 | tf_op jit(solution)/shard_map/all_to_all | solution.py:68
  37.8 10.8 %multiply_reduce_fusion.2 = (f32[256]{0:T(256)S(1)}, f32[256]{0:T(256)S(1)}, f32[256,32,14,14]{0,1,3,2:T(8,128)}) fusion(bf16[1024,256,1,1]{1,0,3,2:T(8,128)(2,1)S(1)} %bitcast.103, bf16[32,14,14,1024]{3,0,2,1:T(8,128)(2,1)} %param.11), kind=kOutput, calls=%fused_computation.7 | convolution fusion | flops 3293150720 | bytes 19793920 | tf_op jit(solution)/shard_map/dot_general | solution.py:73
  48.6 5.1 %all-reduce.6 = (f32[256]{0:T(256)S(1)}, f32[256]{0:T(256)S(1)}) all-reduce(f32[256]{0:T(256)S(1)} %get-tuple-element.12, f32[256]{0:T(256)S(1)} %get-tuple-element.11), channel_id=1, replica_groups=mesh['point'=32,'batch_0'=2,'batch_1'=2] {'batch_0'}, use_global_device_ids=true, to_apply=%region_2.3 | all-reduce | flops 512 | bytes 4096 | tf_op jit(solution)/shard_map/psum | solution.py:15
  53.8 2.4 %all-reduce.3 = (f32[256]{0:T(256)S(1)}, f32[256]{0:T(256)S(1)}) all-reduce(f32[256]{0:T(256)S(1)} %get-tuple-element.25, f32[256]{0:T(256)S(1)} %get-tuple-element.26), channel_id=1, replica_groups=mesh['point'=32,'batch_0'=2,'batch_1'=2] {'batch_1'}, use_global_device_ids=true, to_apply=%region_3.4 | all-reduce | flops 512 | bytes 4096 | tf_op jit(solution)/shard_map/psum | solution.py:15
  56.2 0.6 add_rsqrt_fusion.2
  56.8 4.1 %fusion.1 = bf16[32,14,14,256]{3,0,2,1:T(8,128)(2,1)S(1)} fusion(f32[256,32,14,14]{0,1,3,2:T(8,128)} %get-tuple-element.63, f32[256]{0:T(256)S(1)} %bitcast.110, f32[256]{0:T(256)S(1)} %bitcast.111, f32[256]{0:T(256)S(1)} %get-tuple-element.31, f32[256]{0:T(256)S(1)} %get-tuple-element.57), kind=kLoop, calls=%fused_computation.13 | loop fusion | flops 9633792 | bytes 9637888 | tf_op jit(solution)/shard_map/convert_element_type | solution.py:136
  60.8 4.9 %pad_slice_fusion.2 = (bf16[32,16,14,256]{3,0,2,1:T(8,128)(2,1)}, bf16[32,16,14,256]{3,0,2,1:T(8,128)(2,1)}, bf16[32,16,14,256]{3,0,2,1:T(8,128)(2,1)}) fusion(bf16[32,14,14,256]{3,0,2,1:T(8,128)(2,1)S(1)} %fusion.1), kind=kLoop, calls=%fused_computation.11 | loop fusion | bytes 14221312 | tf_op jit(solution)/shard_map/slice | solution.py:95
  65.8 0.0 copy-done.4
  65.8 0.0 all-to-all-done.1
  65.8 9.8 %all-to-all-start.2 = ((bf16[32,8,1024]{2,1,0:T(8,128)(2,1)}), bf16[32,8,1024]{2,1,0:T(8,128)(2,1)S(1)}, u32[]{:S(2)}, u32[]{:S(2)}) async-start(bf16[32,8,1024]{2,1,0:T(8,128)(2,1)} %add_convert_fusion.2), calls=%async_computation.2 | async-start | bytes 1048576 | tf_op jit(solution)/shard_map/all_to_all | solution.py:68
  75.6 7.3 %fusion.9 = f32[32,14,14,256]{3,0,2,1:T(8,128)} fusion(bf16[2304,256]{1,0:T(8,128)(2,1)S(1)} %bitcast.100, bf16[32,16,14,256]{3,0,2,1:T(8,128)(2,1)} %get-tuple-element.35, bf16[32,16,14,256]{3,0,2,1:T(8,128)(2,1)} %get-tuple-element.34, bf16[32,16,14,256]{3,0,2,1:T(8,128)(2,1)} %get-tuple-element.33), kind=kOutput, calls=%fused_computation.28 | convolution fusion | flops 2499280896 | bytes 17825792 | tf_op jit(solution)/shard_map/dot_general | solution.py:73
  82.9 1.1 copy-done.1
  83.9 1.0 copy-done.2
  85.0 5.4 %fusion.8 = f32[32,14,14,256]{3,0,2,1:T(8,128)} fusion(bf16[2304,256]{1,0:T(8,128)(2,1)S(1)} %bitcast.101, bf16[32,16,14,256]{3,0,2,1:T(8,128)(2,1)S(1)} %copy-done.2, bf16[32,16,14,256]{3,0,2,1:T(8,128)(2,1)S(1)} %copy-done.1, bf16[32,16,14,256]{3,0,2,1:T(8,128)(2,1)S(1)} %copy-done), kind=kOutput, calls=%fused_computation.26 | convolution fusion | flops 2499280896 | bytes 17825792 | tf_op jit(solution)/shard_map/dot_general | solution.py:73
  90.4 8.9 %multiply_reduce_fusion.1 = (f32[256]{0:T(256)S(1)}, f32[256]{0:T(256)S(1)}, f32[32,14,14,256]{3,0,2,1:T(8,128)}) fusion(bf16[2304,256]{1,0:T(8,128)(2,1)S(1)} %bitcast.102, bf16[32,16,14,256]{3,0,2,1:T(8,128)(2,1)S(1)} %copy-done.2, bf16[32,16,14,256]{3,0,2,1:T(8,128)(2,1)S(1)} %copy-done.1, bf16[32,16,14,256]{3,0,2,1:T(8,128)(2,1)S(1)} %copy-done, ...), kind=kOutput, calls=%fused_computation.5 | convolution fusion | flops 2507308544 | bytes 30672896 | tf_op jit(solution)/shard_map/dot_general | solution.py:73
  99.3 4.9 %all-reduce.5 = (f32[256]{0:T(256)S(1)}, f32[256]{0:T(256)S(1)}) all-reduce(f32[256]{0:T(256)S(1)} %get-tuple-element.10, f32[256]{0:T(256)S(1)} %get-tuple-element.9), channel_id=1, replica_groups=mesh['point'=32,'batch_0'=2,'batch_1'=2] {'batch_0'}, use_global_device_ids=true, to_apply=%region_8.9 | all-reduce | flops 512 | bytes 4096 | tf_op jit(solution)/shard_map/psum | solution.py:15
  104.2 2.4 %all-reduce.2 = (f32[256]{0:T(256)S(1)}, f32[256]{0:T(256)S(1)}) all-reduce(f32[256]{0:T(256)S(1)} %get-tuple-element.23, f32[256]{0:T(256)S(1)} %get-tuple-element.24), channel_id=1, replica_groups=mesh['point'=32,'batch_0'=2,'batch_1'=2] {'batch_1'}, use_global_device_ids=true, to_apply=%region_9.10 | all-reduce | flops 512 | bytes 4096 | tf_op jit(solution)/shard_map/psum | solution.py:15
  106.7 0.6 add_rsqrt_fusion.1
  107.3 0.0 all-to-all-done.2
  107.3 9.6 %all-to-all-start.3 = ((bf16[32,1000,32]{1,2,0:T(8,128)(2,1)}), bf16[32,1000,32]{1,2,0:T(8,128)(2,1)S(1)}, u32[]{:S(2)}, u32[]{:S(2)}) async-start(bf16[32,1000,32]{1,2,0:T(8,128)(2,1)} %add_convert_fusion), calls=%async_computation.3 | async-start | bytes 4194304 | tf_op jit(solution)/shard_map/all_to_all | solution.py:66
  116.9 14.0 %multiply_reduce_fusion = (f32[1024]{0:T(1024)S(1)}, f32[1024]{0:T(1024)S(1)}, f32[32,14,14,1024]{3,0,2,1:T(8,128)}) fusion(bf16[32,8,1024]{2,1,0:T(8,128)(2,1)S(1)} %all-to-all-done.2, f32[32,14,14,256]{3,0,2,1:T(8,128)} %get-tuple-element.64, f32[256]{0:T(256)S(1)} %bitcast.116, f32[256]{0:T(256)S(1)} %bitcast.117, f32[256]{0:T(256)S(1)} %get-tuple-element.29, ...), kind=kOutput, calls=%fused_computation.1 | convolution fusion | flops 3317233664 | bytes 32649216 | tf_op jit(solution)/shard_map/dot_general | solution.py:73
  130.9 5.0 %all-reduce.4 = (f32[1024]{0:T(1024)S(1)}, f32[1024]{0:T(1024)S(1)}) all-reduce(f32[1024]{0:T(1024)S(1)} %get-tuple-element.8, f32[1024]{0:T(1024)S(1)} %get-tuple-element.7), channel_id=1, replica_groups=mesh['point'=32,'batch_0'=2,'batch_1'=2] {'batch_0'}, use_global_device_ids=true, to_apply=%region_14.15 | all-reduce | flops 2048 | bytes 16384 | tf_op jit(solution)/shard_map/psum | solution.py:15
  135.9 2.5 %all-reduce.1 = (f32[1024]{0:T(1024)S(1)}, f32[1024]{0:T(1024)S(1)}) all-reduce(f32[1024]{0:T(1024)S(1)} %get-tuple-element.21, f32[1024]{0:T(1024)S(1)} %get-tuple-element.22), channel_id=1, replica_groups=mesh['point'=32,'batch_0'=2,'batch_1'=2] {'batch_1'}, use_global_device_ids=true, to_apply=%region_15.16 | all-reduce | flops 2048 | bytes 16384 | tf_op jit(solution)/shard_map/psum | solution.py:15
  138.4 0.6 add_rsqrt_fusion
  139.0 14.7 %maximum_reduce_fusion = f32[32,1024]{1,0:T(8,128)S(1)} fusion(bf16[32,14,14,1024]{3,0,2,1:T(8,128)(2,1)} %param.11, f32[32,14,14,1024]{3,0,2,1:T(8,128)} %get-tuple-element.65, f32[1024]{0:T(1024)S(1)} %bitcast.106, f32[1024]{0:T(1024)S(1)} %bitcast.107, f32[1024]{0:T(1024)S(1)} %get-tuple-element.27, f32[1024]{0:T(1024)S(1)} %get-tuple-element.52), kind=kLoop, calls=%fused_computation | loop fusion | flops 51347456 | bytes 38682624 | tf_op jit(solution)/shard_map/reduce_sum | solution.py:147
  153.7 0.0 all-to-all-done.3
  153.8 0.6 select_reduce_fusion
  154.4 0.6 subtract_reduce_fusion
  155.6 6.3 %all_to_all.54 = f32[4,1,1]{2,1,0:T(1,128)S(1)} all-to-all(f32[4,1,1]{2,1,0:T(1,128)S(1)} %broadcast_in_dim.46), channel_id=1, replica_groups=mesh['point'=32,'batch_0'=2,'batch_1'=2] {'batch_0','batch_1'}, dimensions={0} | all-to-all | bytes 32 | tf_op jit(solution)/shard_map/all_to_all | solution.py:21
  161.9 0.6 reduce_sum.109
  162.5 0.7 broadcast_in_dim.47
  163.2 25.2 %all_to_all.55 = f32[32,1,1]{2,1,0:T(1,128)S(1)} all-to-all(f32[32,1,1]{2,1,0:T(1,128)S(1)} %broadcast_in_dim.47), channel_id=1, replica_groups=mesh['point'=32,'batch_0'=2,'batch_1'=2] {'point'}, dimensions={0} | all-to-all | bytes 256 | tf_op jit(solution)/shard_map/all_to_all | solution.py:21
  188.4 0.8 reduce.4
  (18 shorter events, 0.1 us)
Async XLA Ops:
  3.3 24.6 %all-to-all-start = ((bf16[32,32,256]{2,1,0:T(8,128)(2,1)}), bf16[32,32,256]{2,1,0:T(8,128)(2,1)S(1)}, u32[]{:S(2)}, u32[]{:S(2)}) async-start(bf16[32,32,256]{2,1,0:T(8,128)(2,1)} %add_convert_fusion.3), calls=%async_computation | async-start | bytes 1048576 | tf_op jit(solution)/shard_map/all_to_all | solution.py:68
  27.9 37.8 %all-to-all-start.1 = ((bf16[32,72,256]{2,1,0:T(8,128)(2,1)}), bf16[32,72,256]{2,1,0:T(8,128)(2,1)S(1)}, u32[]{:S(2)}, u32[]{:S(2)}) async-start(bf16[32,72,256]{2,1,0:T(8,128)(2,1)} %add_convert_fusion.1), calls=%async_computation.1 | async-start | bytes 2359296 | tf_op jit(solution)/shard_map/all_to_all | solution.py:68
  56.8 9.0 %copy-start.4 = (f32[256]{0:T(256)}, f32[256]{0:T(256)S(1)}, u32[]{:S(2)}) copy-start(f32[256]{0:T(256)S(1)} %get-tuple-element.57) | copy-start | bytes 3076
  65.8 41.5 %all-to-all-start.2 = ((bf16[32,8,1024]{2,1,0:T(8,128)(2,1)}), bf16[32,8,1024]{2,1,0:T(8,128)(2,1)S(1)}, u32[]{:S(2)}, u32[]{:S(2)}) async-start(bf16[32,8,1024]{2,1,0:T(8,128)(2,1)} %add_convert_fusion.2), calls=%async_computation.2 | async-start | bytes 1048576 | tf_op jit(solution)/shard_map/all_to_all | solution.py:68
  75.6 7.3 %copy-start = (bf16[32,16,14,256]{3,0,2,1:T(8,128)(2,1)S(1)}, bf16[32,16,14,256]{3,0,2,1:T(8,128)(2,1)}, u32[]{:S(2)}) copy-start(bf16[32,16,14,256]{3,0,2,1:T(8,128)(2,1)} %get-tuple-element.33) | copy-start | bytes 11010052
  75.6 8.4 %copy-start.1 = (bf16[32,16,14,256]{3,0,2,1:T(8,128)(2,1)S(1)}, bf16[32,16,14,256]{3,0,2,1:T(8,128)(2,1)}, u32[]{:S(2)}) copy-start(bf16[32,16,14,256]{3,0,2,1:T(8,128)(2,1)} %get-tuple-element.34) | copy-start | bytes 11010052
  75.6 9.4 %copy-start.2 = (bf16[32,16,14,256]{3,0,2,1:T(8,128)(2,1)S(1)}, bf16[32,16,14,256]{3,0,2,1:T(8,128)(2,1)}, u32[]{:S(2)}) copy-start(bf16[32,16,14,256]{3,0,2,1:T(8,128)(2,1)} %get-tuple-element.35) | copy-start | bytes 11010052
  107.2 23.7 %copy-start.5 = (f32[256]{0:T(256)}, f32[256]{0:T(256)S(1)}, u32[]{:S(2)}) copy-start(f32[256]{0:T(256)S(1)} %get-tuple-element.56) | copy-start | bytes 3076
  107.3 46.5 %all-to-all-start.3 = ((bf16[32,1000,32]{1,2,0:T(8,128)(2,1)}), bf16[32,1000,32]{1,2,0:T(8,128)(2,1)S(1)}, u32[]{:S(2)}, u32[]{:S(2)}) async-start(bf16[32,1000,32]{1,2,0:T(8,128)(2,1)} %add_convert_fusion), calls=%async_computation.3 | async-start | bytes 4194304 | tf_op jit(solution)/shard_map/all_to_all | solution.py:66
  139.0 14.8 %copy-start.3 = (f32[1024]{0:T(1024)}, f32[1024]{0:T(1024)S(1)}, u32[]{:S(2)}) copy-start(f32[1024]{0:T(1024)S(1)} %get-tuple-element.52) | copy-start | bytes 12292
  139.0 14.8 %copy-start.6 = (s32[32]{0:T(128)S(1)}, s32[32]{0:T(128)}, u32[]{:S(2)}) copy-start(s32[32]{0:T(128)} %param.12) | copy-start | bytes 388
where the time goes:
time: 190 us; the launch traced here: 189 us
  blocking collectives  53.9 us (28%)
  matrix products  47.1 us (25%)
  starting transfers between devices  40 us (21%)
  other arithmetic  38.5 us (20%)
  local copies, waits for them, and re-layouts  8.33 us (4%)
    dot_general x5, matrix products, map_product(): lax.dot_general(maps, kernel, (((3,), (0,)), ((), ())), preferred_element...  46.5 us
    all_to_all x2, blocking collectives, sent_to_all(): return lax.all_to_all(copies, axis, split_axis=0, concat_axis=0, tiled=True)  31.5 us
    all_to_all x3, starting transfers between devices, point_weight(): lax.all_to_all(all_points, 'point', split_axis=0, concat_axis=1, tiled=True)  30.3 us
    psum x6, blocking collectives, by_axis(): x = lax.psum(x, axis)  22.4 us
    reduce_sum x1, other arithmetic, shards(): pooled = jnp.mean(block_out, axis=(1, 2)).astype(jnp.bfloat16)  14.7 us
    all_to_all x1, starting transfers between devices, point_weight(): lax.all_to_all(all_points, 'point', split_axis=0, concat_axis=2, tiled=True)  9.65 us
    convert_element_type x4, other arithmetic, point_weight(): all_points = blend_all(coefficients, endpoints).astype(jnp.bfloat16)  6.13 us
    add x2, other arithmetic, blend_all(): return start_part + bend_part + final_part  5.61 us
  transfers between devices with their start and end apart: 4, of which 0 were waited for; matrix products, arithmetic and copies ran while one was open for 45% of the time, Pallas kernels for 0%

commit v1 on v0

v1 whole, which is shorter than its diff:
```python
import jax
import jax.numpy as jnp
from jax import lax
from jax.experimental import pallas as pl
from jax.experimental.pallas import tpu as pltpu
from jax.sharding import Mesh
from jax.sharding import PartitionSpec as P

POINT = ("pz", "px", "py")
BATCH = ("bz", "core")
EPSILON = 1e-05
SM = pl.BlockSpec(memory_space=pltpu.SMEM)
VM = pl.BlockSpec(memory_space=pltpu.VMEM)
HBM = pl.BlockSpec(memory_space=pltpu.HBM)


def coefficients_of(values_ref, index_ref, point):
    doubled = 2.0 * values_ref[index_ref[point]]
    return (
        jnp.maximum(1.0 - doubled, 0.0),
        1.0 - jnp.abs(1.0 - doubled),
        jnp.maximum(doubled - 1.0, 0.0),
    )


def blend(row, parts):
    return row[0] * parts[0] + row[1] * parts[1] + row[2] * parts[2]


def first_weights(t_values, point_index, own, w_reduce, gains, biases, class_bias, lanes):
    _, rows, middle = w_reduce.shape
    points = point_index.shape[0]
    classes = class_bias.shape[1]

    def body(values_ref, index_ref, own_ref, reduce_ref, gains_ref, biases_ref, class_ref,
             out_ref, gain_ref, bias_ref, shift_ref, wide_ref):
        wide_ref[...] = reduce_ref[...].astype(jnp.float32)

        def one(point, carry):
            row = coefficients_of(values_ref, index_ref, point)
            out_ref[point] = blend(row, wide_ref).astype(jnp.bfloat16)
            return carry

        lax.fori_loop(0, points, one, 0)
        row = coefficients_of(values_ref, index_ref, own_ref[0])

        def ends(ref):
            return [ref[k : k + 1, :] for k in range(3)]

        gain_ref[...] = blend(row, ends(gains_ref))
        bias_ref[...] = blend(row, ends(biases_ref))
        shift_ref[...] = jnp.full((1, lanes), -1e30, jnp.float32)
        shift_ref[:, :classes] = blend(row, ends(class_ref))

    return pl.pallas_call(
        body,
        name="first_weights",
        in_specs=[SM, SM, SM, VM, VM, VM, VM],
        out_specs=[VM] * 4,
        out_shape=[
            jax.ShapeDtypeStruct((points, rows, middle), jnp.bfloat16),
            jax.ShapeDtypeStruct((1, gains.shape[1]), jnp.float32),
            jax.ShapeDtypeStruct((1, biases.shape[1]), jnp.float32),
            jax.ShapeDtypeStruct((1, lanes), jnp.float32),
        ],
        scratch_shapes=[pltpu.VMEM(w_reduce.shape, jnp.float32)],
        compiler_params=pltpu.CompilerParams(vmem_limit_bytes=16 << 20),
    )(t_values, point_index, own, w_reduce, gains, biases, class_bias)


def other_weights(t_values, point_index, w_spatial, w_expand, w_classes, lanes):
    _, taps, middle = w_spatial.shape
    _, rows, channels = w_expand.shape
    _, cols, classes = w_classes.shape
    points = point_index.shape[0]
    pieces = channels // middle
    packed = taps + pieces * rows

    def body(values_ref, index_ref, spatial_ref, expand_ref, classes_ref, conv_ref, class_ref,
             packed_ref, wide_ref):
        packed_ref[:, :taps, :] = spatial_ref[...].astype(jnp.float32)
        for piece in range(pieces):
            start = taps + piece * rows
            packed_ref[:, start : start + rows, :] = expand_ref[
                :, :, piece * middle : (piece + 1) * middle
            ].astype(jnp.float32)
        wide_ref[...] = jnp.zeros(wide_ref.shape, jnp.float32)
        wide_ref[:, :, :classes] = classes_ref[...].astype(jnp.float32)

        def one(point, carry):
            row = coefficients_of(values_ref, index_ref, point)
            conv_ref[point] = blend(row, packed_ref).astype(jnp.bfloat16)
            class_ref[point] = blend(row, wide_ref).astype(jnp.bfloat16)
            return carry

        lax.fori_loop(0, points, one, 0)

    return pl.pallas_call(
        body,
        name="other_weights",
        in_specs=[SM, SM, VM, VM, VM],
        out_specs=[VM] * 2,
        out_shape=[
            jax.ShapeDtypeStruct((points, packed, middle), jnp.bfloat16),
            jax.ShapeDtypeStruct((points, cols, lanes), jnp.bfloat16),
        ],
        scratch_shapes=[
            pltpu.VMEM((3, packed, middle), jnp.float32),
            pltpu.VMEM((3, cols, lanes), jnp.float32),
        ],
        compiler_params=pltpu.CompilerParams(vmem_limit_bytes=16 << 20),
    )(t_values, point_index, w_spatial, w_expand, w_classes)


def exchange(x):
    return lax.all_to_all(x, POINT, split_axis=0, concat_axis=0, tiled=True)


def batch_sum(x):
    x = x + lax.ppermute(x, "core", [(0, 1), (1, 0)])
    return x + lax.ppermute(x, "bz", [(0, 1), (1, 0)])


def cost(flops):
    return pl.CostEstimate(flops=flops, transcendentals=0, bytes_accessed=flops // 512)


def column_sums(x):
    return jnp.sum(x.reshape(x.shape[0] // 8, 8, x.shape[1]), axis=0)


def moments(sums, rows):
    mean = sums[0:1] * (1.0 / rows)
    var = sums[1:2] * (1.0 / rows) - mean * mean
    return mean, var


def reduce_stage(maps, weight, side, images):
    rows, channels = maps.shape
    middle = weight.shape[1]
    chunk = side * images

    def body(maps_ref, weight_ref, reduced_ref, sums_ref, held_ref, block_ref, sems, out_sems):
        def copy(step):
            part = pl.ds(step * chunk, chunk)
            return pltpu.make_async_copy(maps_ref.at[part], held_ref.at[part], sems.at[step])

        def copy_out(step):
            part = pl.ds(step * chunk, chunk)
            return pltpu.make_async_copy(
                block_ref.at[part], reduced_ref.at[part], out_sems.at[step]
            )

        for step in range(side):
            copy(step).start()

        def one(step, carry):
            total, squares = carry
            copy(step).wait()
            part = pl.ds(step * chunk, chunk)
            product = jnp.dot(
                held_ref[part, :], weight_ref[...], preferred_element_type=jnp.float32
            )
            block_ref[part, :] = product
            copy_out(step).start()
            return total + column_sums(product), squares + column_sums(product * product)

        zero = jnp.zeros((8, middle), jnp.float32)
        total, squares = lax.fori_loop(0, side, one, (zero, zero))
        sums_ref[0:1, :] = jnp.sum(total, axis=0, keepdims=True)
        sums_ref[1:2, :] = jnp.sum(squares, axis=0, keepdims=True)
        for step in range(side):
            copy_out(step).wait()

    return pl.pallas_call(
        body,
        name="reduce_stage",
        in_specs=[HBM, VM],
        out_specs=[HBM, VM],
        out_shape=[
            pltpu.HBM((rows, middle), jnp.float32),
            jax.ShapeDtypeStruct((2, middle), jnp.float32),
        ],
        scratch_shapes=[
            pltpu.VMEM((rows, channels), jnp.bfloat16),
            pltpu.VMEM((rows, middle), jnp.float32),
            pltpu.SemaphoreType.DMA((side,)),
            pltpu.SemaphoreType.DMA((side,)),
        ],
        compiler_params=pltpu.CompilerParams(vmem_limit_bytes=32 << 20),
        cost_estimate=cost(2 * rows * channels * middle),
    )(maps, weight)


def spatial_stage(reduced, sums, gain, bias, weights, taps, side, images, row_count):
    rows, middle = reduced.shape
    shards_of, packed, _ = weights.shape
    mixed = shards_of * taps
    pieces = 4
    each = (packed - taps) // pieces
    chunk = side * images
    wide = chunk + 2 * images

    def body(reduced_ref, sums_ref, gain_ref, bias_ref, weights_ref, spatial_ref, out_ref,
             mean_ref, var_ref, expand_ref, first_ref, weight_ref, held_ref, sems):
        def copy(step):
            part = pl.ds(step * chunk, chunk)
            return pltpu.make_async_copy(reduced_ref.at[part], held_ref.at[part], sems.at[step])

        for step in range(side):
            copy(step).start()
        mean, var = moments(sums_ref[...], row_count)
        mean_ref[...] = mean
        var_ref[...] = var
        scale = lax.rsqrt(var + EPSILON) * gain_ref[...]
        shift = bias_ref[...] - mean * scale
        weight_ref[...] = (
            weights_ref[:, :taps, :]
            .astype(jnp.float32)
            .reshape(mixed, middle)
            .astype(jnp.bfloat16)
        )
        for piece in range(pieces):
            start = taps + piece * each
            expand_ref[:, piece * middle : (piece + 1) * middle] = (
                weights_ref[:, start : start + each, :]
                .astype(jnp.float32)
                .reshape(shards_of * each, middle)
                .astype(jnp.bfloat16)
            )
        edge = jnp.zeros((images, middle), jnp.bfloat16)
        first_ref[0] = jnp.zeros((wide, middle), jnp.bfloat16)
        first_ref[side + 1] = jnp.zeros((wide, middle), jnp.bfloat16)

        def norm(row, carry):
            copy(row).wait()
            values = held_ref[pl.ds(row * chunk, chunk), :]
            values = jnp.maximum(values * scale + shift, 0.0)
            first_ref[row + 1, 0:images, :] = edge
            first_ref[row + 1, images : images + chunk, :] = values.astype(jnp.bfloat16)
            first_ref[row + 1, images + chunk :, :] = edge
            return carry

        lax.fori_loop(0, side, norm, 0)

        def one(step, carry):
            total, squares = carry
            windows = [
                first_ref[step + dy, dx * images : dx * images + chunk, :]
                for dy in range(3)
                for dx in range(3)
            ]
            product = sum(
                jnp.dot(
                    window,
                    weight_ref[tap * middle : (tap + 1) * middle, :],
                    preferred_element_type=jnp.float32,
                )
                for tap, window in enumerate(windows)
            )
            spatial_ref[pl.ds(step * chunk, chunk), :] = product
            return total + column_sums(product), squares + column_sums(product * product)

        zero = jnp.zeros((8, middle), jnp.float32)
        total, squares = lax.fori_loop(0, side, one, (zero, zero))
        out_ref[0:1, :] = jnp.sum(total, axis=0, keepdims=True)
        out_ref[1:2, :] = jnp.sum(squares, axis=0, keepdims=True)

    return pl.pallas_call(
        body,
        name="spatial_stage",
        in_specs=[HBM] + [VM] * 4,
        out_specs=[VM] * 5,
        out_shape=[
            jax.ShapeDtypeStruct((rows, middle), jnp.float32),
            jax.ShapeDtypeStruct((2, middle), jnp.float32),
            jax.ShapeDtypeStruct((1, middle), jnp.float32),
            jax.ShapeDtypeStruct((1, middle), jnp.float32),
            jax.ShapeDtypeStruct((shards_of * each, pieces * middle), jnp.bfloat16),
        ],
        scratch_shapes=[
            pltpu.VMEM((side + 2, wide, middle), jnp.bfloat16),
            pltpu.VMEM((mixed, middle), jnp.bfloat16),
            pltpu.VMEM((rows, middle), jnp.float32),
            pltpu.SemaphoreType.DMA((side,)),
        ],
        compiler_params=pltpu.CompilerParams(vmem_limit_bytes=24 << 20),
        cost_estimate=cost(2 * rows * mixed * middle),
    )(reduced, sums, gain, bias, weights)


def second_stage(spatial, sums, gain, bias, weight, side, images, row_count):
    rows, middle = spatial.shape
    channels = weight.shape[1]
    chunk = side * images

    def body(spatial_ref, sums_ref, gain_ref, bias_ref, weight_ref, second_ref, out_ref,
             mean_ref, var_ref):
        mean, var = moments(sums_ref[...], row_count)
        mean_ref[...] = mean
        var_ref[...] = var
        scale = lax.rsqrt(var + EPSILON) * gain_ref[...]
        shift = bias_ref[...] - mean * scale

        def one(step, carry):
            total, gram = carry
            part = pl.ds(step * chunk, chunk)
            values = jnp.maximum(spatial_ref[part, :] * scale + shift, 0.0).astype(jnp.bfloat16)
            second_ref[part, :] = values
            gram = gram + lax.dot_general(
                values, values, (((0,), (0,)), ((), ())), preferred_element_type=jnp.float32
            )
            return total + column_sums(values.astype(jnp.float32)), gram

        total, gram = lax.fori_loop(
            0,
            side,
            one,
            (jnp.zeros((8, middle), jnp.float32), jnp.zeros((middle, middle), jnp.float32)),
        )
        stacked = jnp.concatenate([gram, total], axis=0)
        high = stacked.astype(jnp.bfloat16)
        rest = stacked - high.astype(jnp.float32)
        mid = rest.astype(jnp.bfloat16)
        low = (rest - mid.astype(jnp.float32)).astype(jnp.bfloat16)
        kernel = weight_ref[...]
        product = (
            jnp.dot(low, kernel, preferred_element_type=jnp.float32)
            + jnp.dot(mid, kernel, preferred_element_type=jnp.float32)
            + jnp.dot(high, kernel, preferred_element_type=jnp.float32)
        )
        out_ref[0:1, :] = jnp.sum(product[middle:], axis=0, keepdims=True)
        out_ref[1:2, :] = jnp.sum(
            product[:middle] * kernel.astype(jnp.float32), axis=0, keepdims=True
        )

    return pl.pallas_call(
        body,
        name="second_stage",
        in_specs=[VM] * 5,
        out_specs=[VM] * 4,
        out_shape=[
            jax.ShapeDtypeStruct((rows, middle), jnp.bfloat16),
            jax.ShapeDtypeStruct((2, channels), jnp.float32),
            jax.ShapeDtypeStruct((1, middle), jnp.float32),
            jax.ShapeDtypeStruct((1, middle), jnp.float32),
        ],
        compiler_params=pltpu.CompilerParams(vmem_limit_bytes=16 << 20),
        cost_estimate=cost(2 * rows * middle * middle),
    )(spatial, sums, gain, bias, weight)


def output_stage(second, maps, sums, gain, bias, weight, side, images, row_count):
    rows, middle = second.shape
    channels = weight.shape[1]
    chunk = side * images
    tiles = 4
    width = channels // tiles

    def body(second_ref, maps_ref, sums_ref, gain_ref, bias_ref, weight_ref, out_ref, mean_ref,
             var_ref, pooled_ref, held_ref, sems):
        def copy(step):
            part = pl.ds(step * chunk, chunk)
            return pltpu.make_async_copy(maps_ref.at[part], held_ref.at[part], sems.at[step])

        for step in range(side):
            copy(step).start()
        mean, var = moments(sums_ref[...], row_count)
        mean_ref[...] = mean
        var_ref[...] = var
        scale_all = lax.rsqrt(var + EPSILON) * gain_ref[...]
        shift_all = bias_ref[...] - mean * scale_all
        pooled_ref[...] = jnp.zeros((images, channels), jnp.float32)

        def one(step, carry):
            copy(step).wait()
            part = pl.ds(step * chunk, chunk)
            for tile in range(tiles):
                cols = slice(tile * width, (tile + 1) * width)
                product = jnp.dot(
                    second_ref[part, :], weight_ref[:, cols], preferred_element_type=jnp.float32
                )
                values = product * scale_all[:, cols] + (
                    shift_all[:, cols] + held_ref[part, cols].astype(jnp.float32)
                )
                values = jnp.maximum(values, 0.0)
                pooled_ref[:, cols] += jnp.sum(values.reshape(side, images, width), axis=0)
            return carry

        lax.fori_loop(0, side, one, 0)
        out_ref[...] = (pooled_ref[...] * (1.0 / (side * side))).astype(jnp.bfloat16)

    return pl.pallas_call(
        body,
        name="output_stage",
        in_specs=[VM, HBM] + [VM] * 4,
        out_specs=[VM] * 3,
        out_shape=[
            jax.ShapeDtypeStruct((images, channels), jnp.bfloat16),
            jax.ShapeDtypeStruct((1, channels), jnp.float32),
            jax.ShapeDtypeStruct((1, channels), jnp.float32),
        ],
        scratch_shapes=[
            pltpu.VMEM((images, channels), jnp.float32),
            pltpu.VMEM((rows, channels), jnp.bfloat16),
            pltpu.SemaphoreType.DMA((side,)),
        ],
        compiler_params=pltpu.CompilerParams(vmem_limit_bytes=24 << 20),
        cost_estimate=cost(2 * rows * channels * middle),
    )(second, maps, sums, gain, bias, weight)


def probe_stage(pooled, class_w, shift, labels, image_count):
    images, channels = pooled.shape
    lanes = class_w.shape[1]

    def body(labels_ref, pooled_ref, class_ref, shift_ref, margin_ref):
        logits = (
            jnp.dot(pooled_ref[...], class_ref[...], preferred_element_type=jnp.float32)
            + shift_ref[...]
        )
        index = lax.broadcasted_iota(jnp.int32, (images, 1), 0)
        column = jnp.zeros((images, 1), jnp.int32)
        for image in range(images):
            column = jnp.where(index == image, labels_ref[image], column)
        onehot = lax.broadcasted_iota(jnp.int32, (images, lanes), 1) == column
        correct = jnp.sum(jnp.where(onehot, logits, 0.0), axis=1, keepdims=True)
        rivals = jnp.max(jnp.where(onehot, -1e30, logits), axis=1, keepdims=True)
        total = jnp.sum(correct - rivals, axis=0, keepdims=True) * (1.0 / image_count)
        margin_ref[...] = jnp.broadcast_to(total, (1, 128))

    return pl.pallas_call(
        body,
        name="probe_stage",
        in_specs=[SM, VM, VM, VM],
        out_specs=VM,
        out_shape=jax.ShapeDtypeStruct((1, 128), jnp.float32),
        compiler_params=pltpu.CompilerParams(vmem_limit_bytes=8 << 20),
    )(labels, pooled, class_w, shift)


def shards(activations, labels, t_values, point_index, w_reduce, w_spatial, w_expand, w_classes,
           norm_gain, norm_bias, class_bias):
    images, side, _, channels = activations.shape
    middle = w_reduce.shape[2]
    image_count = images * lax.axis_size(BATCH)
    row_count = float(image_count * side * side)
    lanes = -(-class_bias.shape[1] // 128) * 128
    own = jnp.reshape(lax.axis_index(POINT), (1,)).astype(jnp.int32)
    sent, gain, bias, shift = first_weights(
        t_values, point_index, own, w_reduce, norm_gain, norm_bias, class_bias, lanes
    )
    reduce_w = exchange(sent).reshape(channels, middle)
    packed, class_sent = other_weights(
        t_values, point_index, w_spatial, w_expand, jnp.swapaxes(w_classes, 1, 2), lanes
    )
    packed, reduce_w = lax.optimization_barrier((packed, reduce_w))
    weights = exchange(packed)
    maps = jnp.transpose(activations, (1, 2, 0, 3)).reshape(side * side * images, channels)
    maps = pltpu.with_memory_space_constraint(maps, pltpu.HBM)
    reduced, sums = reduce_stage(maps, reduce_w, side, images)
    class_sent, sums = lax.optimization_barrier((class_sent, sums))
    class_w = exchange(class_sent).reshape(channels, lanes)
    sums = batch_sum(sums)
    reduced = pltpu.with_memory_space_constraint(reduced, pltpu.HBM)
    spatial, sums, mean_one, var_one, expand_w = spatial_stage(
        reduced, sums, gain[:, :middle], bias[:, :middle], weights, w_spatial.shape[1], side,
        images, row_count
    )
    sums = batch_sum(sums)
    second, sums, mean_two, var_two = second_stage(
        spatial, sums, gain[:, middle : 2 * middle], bias[:, middle : 2 * middle], expand_w,
        side, images, row_count
    )
    sums = batch_sum(sums)
    pooled, mean_three, var_three = output_stage(
        second, maps, sums, gain[:, 2 * middle :], bias[:, 2 * middle :], expand_w, side, images,
        row_count
    )
    margin = probe_stage(pooled, class_w, shift, labels, image_count)
    margin = batch_sum(margin)
    points = lax.axis_size(POINT)
    copies = jnp.broadcast_to(margin[None], (points, 1, 128))
    margin_all = exchange(copies)[:, 0, 0]
    return mean_one, var_one, mean_two, var_two, mean_three, var_three, margin_all


def solution(mesh):
    torus = Mesh(mesh.devices.reshape(2, 4, 4, 2, 2), POINT + BATCH)
    rows = P(POINT, None)
    return jax.shard_map(
        shards,
        mesh=torus,
        in_specs=(
            P(BATCH, None, None, None),
            P(BATCH),
            P(),
            P(),
            P(None, POINT, None),
            P(None, POINT, None),
            P(None, POINT, None),
            P(None, None, POINT),
            P(),
            P(),
            P(),
        ),
        out_specs=(rows, rows, rows, rows, rows, rows, P()),
        check_vma=False,
    )
```

time: 190 us -> 155 us (0.82)
  matrix products: 47.1 us -> 0 us
  Pallas kernels: 0 us -> 39.9 us
  other arithmetic: 38.5 us -> 0.03 us
  waiting for transfers between devices: 0.01 us -> 36 us
  blocking collectives: 53.9 us -> 37.1 us
  starting transfers between devices: 40 us -> 26.1 us
  local copies, waits for them, and re-layouts: 8.33 us -> 14.3 us
    dot_general x6 -> x0, matrix products: 47.1 us -> none  [the longest x5 46.5 us: map_product(): lax.dot_general(maps, kernel, (((3,), (0,)), ((), ())), preferred_element...]
    pallas_call x0 -> x7, Pallas kernels: none -> 39.9 us  [the longest x1 12.9 us: spatial_stage(): pl.pallas_call(body, name='spatial_stage', in_specs=[HBM] + [VM] * 4, out...]
    psum x6 -> x0, blocking collectives: 22.4 us -> none  [by_axis(): x = lax.psum(x, axis)]
    all_to_all x4 -> x3, waiting for transfers between devices: 0.01 us -> 20.8 us  [exchange(): return lax.all_to_all(x, POINT, split_axis=0, concat_axis=0, tiled=True)]
    all_to_all x4 -> x3, starting transfers between devices: 40 us -> 21.7 us  [exchange(): return lax.all_to_all(x, POINT, split_axis=0, concat_axis=0, tiled=True)]
    reduce_sum x4 -> x0, other arithmetic: 16.8 us -> none  [the longest x1 14.7 us: shards(): pooled = jnp.mean(block_out, axis=(1, 2)).astype(jnp.bfloat16)]
    ppermute x0 -> x8, waiting for transfers between devices: none -> 15.2 us  [the longest x4 10.6 us: batch_sum(): return x + lax.ppermute(x, 'bz', [(0, 1), (1, 0)])]
    unnamed x14 -> x32, local copies, waits for them, and re-layouts: 2.13 us -> 13.5 us
  transfers between devices with their start and end apart: 4 -> 11, of which waited for: 0 -> 10; matrix products, arithmetic and copies ran while one was open for 45% -> 0% of each run, Pallas kernels for 0% -> 24%
where the time goes in v1:
time: 155 us; the launch traced here: 154 us
  Pallas kernels  39.9 us (26%)
  blocking collectives  37.1 us (24%)
  waiting for transfers between devices  36 us (23%)
  starting transfers between devices  26.1 us (17%)
  local copies, waits for them, and re-layouts  14.3 us (9%)
    all_to_all x1, blocking collectives, exchange(): return lax.all_to_all(x, POINT, split_axis=0, concat_axis=0, tiled=True)  37.1 us
    all_to_all x3, starting transfers between devices, exchange(): return lax.all_to_all(x, POINT, split_axis=0, concat_axis=0, tiled=True)  21.7 us
    all_to_all x3, waiting for transfers between devices, exchange(): return lax.all_to_all(x, POINT, split_axis=0, concat_axis=0, tiled=True)  20.8 us
    unnamed x32, local copies, waits for them, and re-layouts  13.5 us
    pallas_call x1, Pallas kernels, spatial_stage(): pl.pallas_call(body, name='spatial_stage', in_specs=[HBM] + [VM] * 4, out...  12.9 us
    ppermute x4, waiting for transfers between devices, batch_sum(): return x + lax.ppermute(x, 'bz', [(0, 1), (1, 0)])  10.6 us
    pallas_call x1, Pallas kernels, output_stage(): pl.pallas_call(body, name='output_stage', in_specs=[VM, HBM] + [VM] * 4,...  8.42 us
    pallas_call x1, Pallas kernels, reduce_stage(): pl.pallas_call(body, name='reduce_stage', in_specs=[HBM, VM], out_specs=[...  7.98 us
  transfers between devices with their start and end apart: 11, of which 10 were waited for; matrix products, arithmetic and copies ran while one was open for 0% of the time, Pallas kernels for 24%

profile of v1, /device:TPU:0, one launch (start us, length us, event | category | flops | bytes accessed | tf_op | source)
XLA Modules:
  0.0 154.3 jit_solution(13231508273508258361)
XLA Ops:
  0.7 0.8 copy-done.6
  1.4 0.7 copy-done.8
  2.2 0.7 copy-done.9
  2.9 0.7 copy-done.10
  3.6 0.7 copy-done.11
  4.3 0.7 copy-done.13
  4.9 2.0 %first_weights.1 = (bf16[32,32,256]{2,1,0:T(8,128)(2,1)}, f32[1,1536]{1,0:T(1,128)S(1)}, f32[1,1536]{1,0:T(1,128)S(1)}, f32[1,1024]{1,0:T(1,128)S(1)}) custom-call(f32[64]{0:T(128)S(1)} %copy-done.11, s32[32]{0:T(128)S(1)} %copy-done.13, s32[1]{0:T(128)} %bitcast.3.own_ref, bf16[3,32,256]{2,1,0:T(8,128)(2,1)S(1)} %copy-done.6, f32[3,1536]{1,0:T(4,128)S(1)} %copy-done.8, ...), custom_call_target="tpu_custom_call" | custom-call | tf_op jit(solution)/shard_map/first_weights/pallas_call | solution.py:55
  6.9 10.7 %all-to-all-start = ((bf16[32,32,256]{2,1,0:T(8,128)(2,1)}), bf16[32,32,256]{2,1,0:T(8,128)(2,1)S(1)}, u32[]{:S(2)}, u32[]{:S(2)}) async-start(bf16[32,32,256]{2,1,0:T(8,128)(2,1)} %get-tuple-element.32), calls=%async_computation | async-start | bytes 1048576 | tf_op jit(solution)/shard_map/all_to_all | solution.py:116
  17.6 0.0 copy-start.4
  17.7 0.9 copy-done.4
  18.6 0.9 copy-done.5
  19.5 0.8 copy-done.7
  20.3 0.7 copy-done.12
  20.9 0.7 copy-done.14
  21.6 2.3 %other_weights.1 = (bf16[32,104,256]{2,1,0:T(8,128)(2,1)S(1)}, bf16[32,32,1024]{2,1,0:T(8,128)(2,1)S(1)}) custom-call(f32[64]{0:T(128)S(1)} %copy-done.12, s32[32]{0:T(128)S(1)} %copy-done.14, bf16[3,72,256]{2,1,0:T(8,128)(2,1)S(1)} %copy-done.5, bf16[3,8,1024]{2,1,0:T(8,128)(2,1)S(1)} %copy-done.7, bf16[3,32,1000]{2,1,0:T(8,128)(2,1)S(1)} %bitcast.11), custom_call_target="tpu_custom_call" | custom-call | tf_op jit(solution)/shard_map/other_weights/pallas_call | solution.py:98
  23.9 1.4 copy-done
  25.4 1.2 copy-done.3
  26.6 4.2 %all-to-all-done = bf16[32,32,256]{2,1,0:T(8,128)(2,1)S(1)} async-done(((bf16[32,32,256]{2,1,0:T(8,128)(2,1)}), bf16[32,32,256]{2,1,0:T(8,128)(2,1)S(1)}, u32[]{:S(2)}, u32[]{:S(2)}) %all-to-all-start) | async-done | bytes 524320 | tf_op jit(solution)/shard_map/all_to_all | solution.py:116
  30.8 5.6 %all-to-all-start.1 = ((bf16[32,104,256]{2,1,0:T(8,128)(2,1)}), bf16[32,104,256]{2,1,0:T(8,128)(2,1)S(1)}, u32[]{:S(2)}, u32[]{:S(2)}) async-start(bf16[32,104,256]{2,1,0:T(8,128)(2,1)} %copy-done.3), calls=%async_computation.1 | async-start | bytes 3407872 | tf_op jit(solution)/shard_map/all_to_all | solution.py:116
  36.4 8.0 %reduce_stage.1 = (f32[6272,256]{1,0:T(8,128)}, f32[2,256]{1,0:T(2,128)S(1)}) custom-call(bf16[6272,1024]{1,0:T(8,128)(2,1)} %bitcast.12, bf16[1024,256]{1,0:T(8,128)(2,1)S(1)} %bitcast.10), custom_call_target="tpu_custom_call" | custom-call | flops 3288334336 | bytes 6422528 | tf_op jit(solution)/shard_map/reduce_stage/pallas_call | solution.py:175
  44.4 16.6 %all-to-all-done.1.weights_ref = bf16[32,104,256]{2,1,0:T(8,128)(2,1)S(1)} async-done(((bf16[32,104,256]{2,1,0:T(8,128)(2,1)}), bf16[32,104,256]{2,1,0:T(8,128)(2,1)S(1)}, u32[]{:S(2)}, u32[]{:S(2)}) %all-to-all-start.1) | async-done | bytes 1703968 | tf_op jit(solution)/shard_map/all_to_all | solution.py:116
  61.0 1.2 copy-done.1
  62.2 5.3 %all-to-all-start.2 = ((bf16[32,32,1024]{2,1,0:T(8,128)(2,1)}), bf16[32,32,1024]{2,1,0:T(8,128)(2,1)S(1)}, u32[]{:S(2)}, u32[]{:S(2)}) async-start(bf16[32,32,1024]{2,1,0:T(8,128)(2,1)} %copy-done), calls=%async_computation.2 | async-start | bytes 4194304 | tf_op jit(solution)/shard_map/all_to_all | solution.py:116
  67.5 0.1 collective-permute-start
  67.6 1.1 collective-permute-done
  68.8 1.0 collective-permute-start.1
  69.8 2.7 %collective-permute-done.1 = f32[2,256]{1,0:T(2,128)S(1)} collective-permute-done((f32[2,256]{1,0:T(2,128)S(1)}, f32[2,256]{1,0:T(2,128)S(1)}, u32[]{:S(2)}, u32[]{:S(2)}) %collective-permute-start.1) | collective-permute-done | bytes 2080 | tf_op jit(solution)/shard_map/ppermute | solution.py:121
  72.5 1.5 copy-done.2
  73.9 12.9 %spatial_stage.1 = (f32[6272,256]{1,0:T(8,128)S(1)}, f32[2,256]{1,0:T(2,128)S(1)}, f32[1,256]{1,0:T(1,128)}, f32[1,256]{1,0:T(1,128)}, bf16[256,1024]{1,0:T(8,128)(2,1)S(1)}) custom-call(f32[6272,256]{1,0:T(8,128)} %get-tuple-element.34.reduced_ref, f32[2,256]{1,0:T(2,128)S(1)} %add.33.sums_ref, f32[1,256]{1,0:T(1,128)S(1)} %get-tuple-element.59.gain_ref, ...), custom_call_target="tpu_custom_call" | custom-call | flops 7398752256 | bytes 14450688 | tf_op jit(solution)/shard_map/spatial_stage/pallas_call | solution.py:269
  86.8 0.1 collective-permute-start.2
  86.9 1.1 collective-permute-done.2
  88.1 1.0 collective-permute-start.3
  89.1 2.7 %collective-permute-done.3 = f32[2,256]{1,0:T(2,128)S(1)} collective-permute-done((f32[2,256]{1,0:T(2,128)S(1)}, f32[2,256]{1,0:T(2,128)S(1)}, u32[]{:S(2)}, u32[]{:S(2)}) %collective-permute-start.3) | collective-permute-done | bytes 2080 | tf_op jit(solution)/shard_map/ppermute | solution.py:121
  91.8 5.2 %second_stage.1 = (bf16[6272,256]{1,0:T(8,128)(2,1)S(1)}, f32[2,1024]{1,0:T(2,128)S(1)}, f32[1,256]{1,0:T(1,128)}, f32[1,256]{1,0:T(1,128)}) custom-call(f32[6272,256]{1,0:T(8,128)S(1)} %get-tuple-element.43.spatial_ref, f32[2,256]{1,0:T(2,128)S(1)} %add.35.sums_ref, f32[1,256]{1,0:T(1,128)S(1)} %get-tuple-element.60.gain_ref, ...), custom_call_target="tpu_custom_call" | custom-call | flops 822083584 | bytes 1605632 | tf_op jit(solution)/shard_map/second_stage/pallas_call | solution.py:337
  97.0 0.1 collective-permute-start.4
  97.1 1.2 collective-permute-done.4
  98.3 1.0 collective-permute-start.5
  99.3 2.6 %collective-permute-done.5 = f32[2,1024]{1,0:T(2,128)S(1)} collective-permute-done((f32[2,1024]{1,0:T(2,128)S(1)}, f32[2,1024]{1,0:T(2,128)S(1)}, u32[]{:S(2)}, u32[]{:S(2)}) %collective-permute-start.5) | collective-permute-done | bytes 8224 | tf_op jit(solution)/shard_map/ppermute | solution.py:121
  102.0 8.4 %output_stage.1 = (bf16[32,1024]{1,0:T(8,128)(2,1)S(1)}, f32[1,1024]{1,0:T(1,128)}, f32[1,1024]{1,0:T(1,128)}) custom-call(bf16[6272,256]{1,0:T(8,128)(2,1)S(1)} %get-tuple-element.48.second_ref, bf16[6272,1024]{1,0:T(8,128)(2,1)} %bitcast.13, f32[2,1024]{1,0:T(2,128)S(1)} %add.37.sums_ref, f32[1,1024]{1,0:T(1,128)S(1)} %slice.25.gain_ref, ...), custom_call_target="tpu_custom_call" | custom-call | flops 3288334336 | bytes 6422528 | tf_op jit(solution)/shard_map/output_stage/pallas_call | solution.py:393
  110.4 0.0 all-to-all-done.2
  110.4 0.0 copy-done.15
  110.4 1.1 probe_stage.1
  111.5 0.1 collective-permute-start.6
  111.6 1.1 collective-permute-done.6
  112.8 1.0 collective-permute-start.7
  113.8 2.6 %collective-permute-done.7 = f32[1,128]{1,0:T(1,128)S(1)} collective-permute-done((f32[1,128]{1,0:T(1,128)S(1)}, f32[1,128]{1,0:T(1,128)S(1)}, u32[]{:S(2)}, u32[]{:S(2)}) %collective-permute-start.7) | collective-permute-done | bytes 544 | tf_op jit(solution)/shard_map/ppermute | solution.py:121
  116.3 37.1 %all_to_all.20 = f32[32,1,128]{2,1,0:T(1,128)S(1)} all-to-all(f32[32,1,128]{2,1,0:T(1,128)S(1)} %broadcast_in_dim.9), channel_id=1, replica_groups=mesh['pz'=2,'px'=4,'py'=4,'bz'=2,'core'=2] {'pz','px','py'}, dimensions={0} | all-to-all | bytes 32768 | tf_op jit(solution)/shard_map/all_to_all | solution.py:116
  153.4 0.8 slice_reduce_fusion
  (27 shorter events, 0.1 us)
Async XLA Ops:
  0.6 0.8 copy-start.6
  1.4 0.7 copy-start.8
  2.2 0.7 copy-start.9
  2.9 0.7 copy-start.10
  3.6 0.7 copy-start.11
  4.3 0.7 copy-start.13
  6.9 23.9 %all-to-all-start = ((bf16[32,32,256]{2,1,0:T(8,128)(2,1)}), bf16[32,32,256]{2,1,0:T(8,128)(2,1)S(1)}, u32[]{:S(2)}, u32[]{:S(2)}) async-start(bf16[32,32,256]{2,1,0:T(8,128)(2,1)} %get-tuple-element.32), calls=%async_computation | async-start | bytes 1048576 | tf_op jit(solution)/shard_map/all_to_all | solution.py:116
  17.6 0.9 copy-start.4
  18.6 0.9 copy-start.5
  19.5 0.8 copy-start.7
  20.3 0.7 copy-start.12
  20.9 0.7 copy-start.14
  23.9 1.4 copy-start
  25.3 1.2 copy-start.3
  30.8 30.2 %all-to-all-start.1 = ((bf16[32,104,256]{2,1,0:T(8,128)(2,1)}), bf16[32,104,256]{2,1,0:T(8,128)(2,1)S(1)}, u32[]{:S(2)}, u32[]{:S(2)}) async-start(bf16[32,104,256]{2,1,0:T(8,128)(2,1)} %copy-done.3), calls=%async_computation.1 | async-start | bytes 3407872 | tf_op jit(solution)/shard_map/all_to_all | solution.py:116
  61.0 1.2 copy-start.1
  62.2 48.2 %all-to-all-start.2 = ((bf16[32,32,1024]{2,1,0:T(8,128)(2,1)}), bf16[32,32,1024]{2,1,0:T(8,128)(2,1)S(1)}, u32[]{:S(2)}, u32[]{:S(2)}) async-start(bf16[32,32,1024]{2,1,0:T(8,128)(2,1)} %copy-done), calls=%async_computation.2 | async-start | bytes 4194304 | tf_op jit(solution)/shard_map/all_to_all | solution.py:116
  67.5 1.2 collective-permute-start
  68.8 3.7 %collective-permute-start.1 = (f32[2,256]{1,0:T(2,128)S(1)}, f32[2,256]{1,0:T(2,128)S(1)}, u32[]{:S(2)}, u32[]{:S(2)}) collective-permute-start(f32[2,256]{1,0:T(2,128)S(1)} %add.32), channel_id=1, source_target_pairs={{0,2},{2,0},{1,3},{3,1},{4,6},{6,4},{5,7},{7,5},{8,10},{10,8},{9,1... | collective-permute-start | bytes 6152 | tf_op jit(solution)/shard_map/ppermute | solution.py:121
  72.5 1.5 copy-start.2
  86.8 1.2 collective-permute-start.2
  88.1 3.7 %collective-permute-start.3 = (f32[2,256]{1,0:T(2,128)S(1)}, f32[2,256]{1,0:T(2,128)S(1)}, u32[]{:S(2)}, u32[]{:S(2)}) collective-permute-start(f32[2,256]{1,0:T(2,128)S(1)} %add.34), channel_id=1, source_target_pairs={{0,2},{2,0},{1,3},{3,1},{4,6},{6,4},{5,7},{7,5},{8,10},{10,8},{9,1... | collective-permute-start | bytes 6152 | tf_op jit(solution)/shard_map/ppermute | solution.py:121
  97.0 1.3 collective-permute-start.4
  98.3 3.7 %collective-permute-start.5 = (f32[2,1024]{1,0:T(2,128)S(1)}, f32[2,1024]{1,0:T(2,128)S(1)}, u32[]{:S(2)}, u32[]{:S(2)}) collective-permute-start(f32[2,1024]{1,0:T(2,128)S(1)} %add.36), channel_id=1, source_target_pairs={{0,2},{2,0},{1,3},{3,1},{4,6},{6,4},{5,7},{7,5},{8,10},{10,8},{9,1... | collective-permute-start | bytes 24584 | tf_op jit(solution)/shard_map/ppermute | solution.py:121
  102.0 8.4 %copy-start.15 = (s32[32]{0:T(128)S(1)}, s32[32]{0:T(128)}, u32[]{:S(2)}) copy-start(s32[32]{0:T(128)} %labels_ref.1) | copy-start | bytes 388
  111.5 1.2 collective-permute-start.6
  112.8 3.6 %collective-permute-start.7 = (f32[1,128]{1,0:T(1,128)S(1)}, f32[1,128]{1,0:T(1,128)S(1)}, u32[]{:S(2)}, u32[]{:S(2)}) collective-permute-start(f32[1,128]{1,0:T(1,128)S(1)} %add.38), channel_id=1, source_target_pairs={{0,2},{2,0},{1,3},{3,1},{4,6},{6,4},{5,7},{7,5},{8,10},{10,8},{9,1... | collective-permute-start | bytes 1544 | tf_op jit(solution)/shard_map/ppermute | solution.py:121

commit v2 on v1

--- a/solution.py
+++ b/solution.py
@@ -27,13 +27,32 @@
     return row[0] * parts[0] + row[1] * parts[1] + row[2] * parts[2]
 
 
+def fetch(pairs, sems):
+    copies = [
+        pltpu.make_async_copy(source, target, sems.at[k])
+        for k, (source, target) in enumerate(pairs)
+    ]
+    for copy in copies:
+        copy.start()
+    for copy in copies:
+        copy.wait()
+
+
+def in_hbm(*arrays):
+    return [pltpu.with_memory_space_constraint(x, pltpu.HBM) for x in arrays]
+
+
 def first_weights(t_values, point_index, own, w_reduce, gains, biases, class_bias, lanes):
     _, rows, middle = w_reduce.shape
     points = point_index.shape[0]
     classes = class_bias.shape[1]
 
-    def body(values_ref, index_ref, own_ref, reduce_ref, gains_ref, biases_ref, class_ref,
-             out_ref, gain_ref, bias_ref, shift_ref, wide_ref):
+    def body(own_ref, *refs):
+        sources = refs[:6]
+        out_ref, gain_ref, bias_ref, shift_ref = refs[6:10]
+        values_ref, index_ref, reduce_ref, gains_ref, biases_ref, class_ref = refs[10:16]
+        wide_ref, sems = refs[16:]
+        fetch(list(zip(sources, refs[10:16])), sems)
         wide_ref[...] = reduce_ref[...].astype(jnp.float32)
 
         def one(point, carry):
@@ -55,7 +74,7 @@
     return pl.pallas_call(
         body,
         name="first_weights",
-        in_specs=[SM, SM, SM, VM, VM, VM, VM],
+        in_specs=[SM] + [HBM] * 6,
         out_specs=[VM] * 4,
         out_shape=[
             jax.ShapeDtypeStruct((points, rows, middle), jnp.bfloat16),
@@ -63,53 +82,101 @@
             jax.ShapeDtypeStruct((1, biases.shape[1]), jnp.float32),
             jax.ShapeDtypeStruct((1, lanes), jnp.float32),
         ],
-        scratch_shapes=[pltpu.VMEM(w_reduce.shape, jnp.float32)],
+        scratch_shapes=[
+            pltpu.SMEM(t_values.shape, jnp.float32),
+            pltpu.SMEM(point_index.shape, jnp.int32),
+            pltpu.VMEM(w_reduce.shape, w_reduce.dtype),
+            pltpu.VMEM(gains.shape, jnp.float32),
+            pltpu.VMEM(biases.shape, jnp.float32),
+            pltpu.VMEM(class_bias.shape, jnp.float32),
+            pltpu.VMEM(w_reduce.shape, jnp.float32),
+            pltpu.SemaphoreType.DMA((6,)),
+        ],
         compiler_params=pltpu.CompilerParams(vmem_limit_bytes=16 << 20),
-    )(t_values, point_index, own, w_reduce, gains, biases, class_bias)
-
-
-def other_weights(t_values, point_index, w_spatial, w_expand, w_classes, lanes):
+    )(own, *in_hbm(t_values, point_index, w_reduce, gains, biases, class_bias))
+
+
+def other_weights(t_values, point_index, own, w_spatial, w_expand, w_classes, lanes):
     _, taps, middle = w_spatial.shape
     _, rows, channels = w_expand.shape
     _, cols, classes = w_classes.shape
     points = point_index.shape[0]
-    pieces = channels // middle
-    packed = taps + pieces * rows
-
-    def body(values_ref, index_ref, spatial_ref, expand_ref, classes_ref, conv_ref, class_ref,
-             packed_ref, wide_ref):
-        packed_ref[:, :taps, :] = spatial_ref[...].astype(jnp.float32)
-        for piece in range(pieces):
-            start = taps + piece * rows
-            packed_ref[:, start : start + rows, :] = expand_ref[
-                :, :, piece * middle : (piece + 1) * middle
-            ].astype(jnp.float32)
+    lane = middle // 2
+    tiles = channels // (2 * lane)
+    class_tiles = lanes // (2 * lane)
+    conv_rows = taps + tiles * rows
+    packed = conv_rows + class_tiles * cols
+    groups = 4
+    each = points // groups
+
+    def body(own_ref, values_in, index_in, spatial_in, expand_in, classes_in, out_ref,
+             values_ref, index_ref, spatial_ref, expand_ref, classes_ref, packed_ref, wide_ref,
+             block_ref, sems, out_sems):
+        fetch(
+            [
+                (values_in, values_ref),
+                (index_in, index_ref),
+                (spatial_in, spatial_ref),
+                (expand_in, expand_ref),
+                (classes_in, classes_ref),
+            ],
+            sems,
+        )
+        low = own_ref[1] == 0
         wide_ref[...] = jnp.zeros(wide_ref.shape, jnp.float32)
         wide_ref[:, :, :classes] = classes_ref[...].astype(jnp.float32)
 
+        def half(ref, tile, tiles_of):
+            first = ref[:, :, tile * lane : (tile + 1) * lane].astype(jnp.float32)
+            start = (tiles_of + tile) * lane
+            last = ref[:, :, start : start + lane].astype(jnp.float32)
+            return jnp.where(low, first, last)
+
+        packed_ref[:, :taps, :] = half(spatial_ref, 0, 1)
+        for tile in range(tiles):
+            start = taps + tile * rows
+            packed_ref[:, start : start + rows, :] = half(expand_ref, tile, tiles)
+        for tile in range(class_tiles):
+            start = conv_rows + tile * cols
+            packed_ref[:, start : start + cols, :] = half(wide_ref, tile, class_tiles)
+
+        def copy_out(group):
+            part = pl.ds(group * each, each)
+            return pltpu.make_async_copy(
+                block_ref.at[part], out_ref.at[part], out_sems.at[group]
+            )
+
         def one(point, carry):
             row = coefficients_of(values_ref, index_ref, point)
-            conv_ref[point] = blend(row, packed_ref).astype(jnp.bfloat16)
-            class_ref[point] = blend(row, wide_ref).astype(jnp.bfloat16)
+            block_ref[point] = blend(row, packed_ref).astype(jnp.bfloat16)
             return carry
 
-        lax.fori_loop(0, points, one, 0)
+        for group in range(groups):
+            lax.fori_loop(group * each, (group + 1) * each, one, 0)
+            copy_out(group).start()
+        for group in range(groups):
+            copy_out(group).wait()
 
     return pl.pallas_call(
         body,
         name="other_weights",
-        in_specs=[SM, SM, VM, VM, VM],
-        out_specs=[VM] * 2,
-        out_shape=[
-            jax.ShapeDtypeStruct((points, packed, middle), jnp.bfloat16),
-            jax.ShapeDtypeStruct((points, cols, lanes), jnp.bfloat16),
-        ],
+        in_specs=[SM] + [HBM] * 5,
+        out_specs=HBM,
+        out_shape=pltpu.HBM((points, packed, lane), jnp.bfloat16),
         scratch_shapes=[
-            pltpu.VMEM((3, packed, middle), jnp.float32),
+            pltpu.SMEM(t_values.shape, jnp.float32),
+            pltpu.SMEM(point_index.shape, jnp.int32),
+            pltpu.VMEM(w_spatial.shape, w_spatial.dtype),
+            pltpu.VMEM(w_expand.shape, w_expand.dtype),
+            pltpu.VMEM(w_classes.shape, w_classes.dtype),
+            pltpu.VMEM((3, packed, lane), jnp.float32),
             pltpu.VMEM((3, cols, lanes), jnp.float32),
+            pltpu.VMEM((points, packed, lane), jnp.bfloat16),
+            pltpu.SemaphoreType.DMA((5,)),
+            pltpu.SemaphoreType.DMA((groups,)),
         ],
         compiler_params=pltpu.CompilerParams(vmem_limit_bytes=16 << 20),
-    )(t_values, point_index, w_spatial, w_expand, w_classes)
+    )(own, *in_hbm(t_values, point_index, w_spatial, w_expand, w_classes))
 
 
 def exchange(x):
@@ -192,42 +259,44 @@
     )(maps, weight)
 
 
-def spatial_stage(reduced, sums, gain, bias, weights, taps, side, images, row_count):
+def spatial_stage(own, reduced, sums, gain, bias, mine, other, taps, expand_rows, side, images,
+                  row_count):
     rows, middle = reduced.shape
-    shards_of, packed, _ = weights.shape
+    shards_of, _, lane = mine.shape
     mixed = shards_of * taps
     pieces = 4
-    each = (packed - taps) // pieces
+    each = expand_rows
+    packed = taps + pieces * each
     chunk = side * images
     wide = chunk + 2 * images
 
-    def body(reduced_ref, sums_ref, gain_ref, bias_ref, weights_ref, spatial_ref, out_ref,
-             mean_ref, var_ref, expand_ref, first_ref, weight_ref, held_ref, sems):
+    def body(own_ref, reduced_ref, mine_ref, other_ref, sums_ref, gain_ref, bias_ref,
+             spatial_ref, out_ref, mean_ref, var_ref, expand_ref, first_ref, weight_ref, held_ref,
+             halves_ref, sems, half_sems):
+        core = own_ref[1]
+        rows_of = pl.ds(0, packed)
+        halves = [
+            pltpu.make_async_copy(
+                mine_ref.at[:, rows_of, :], halves_ref.at[core], half_sems.at[0]
+            ),
+            pltpu.make_async_copy(
+                other_ref.at[:, rows_of, :], halves_ref.at[1 - core], half_sems.at[1]
+            ),
+        ]
+
         def copy(step):
             part = pl.ds(step * chunk, chunk)
             return pltpu.make_async_copy(reduced_ref.at[part], held_ref.at[part], sems.at[step])
 
         for step in range(side):
             copy(step).start()
+        for half in halves:
+            half.start()
         mean, var = moments(sums_ref[...], row_count)
         mean_ref[...] = mean
         var_ref[...] = var
         scale = lax.rsqrt(var + EPSILON) * gain_ref[...]
         shift = bias_ref[...] - mean * scale
-        weight_ref[...] = (
-            weights_ref[:, :taps, :]
-            .astype(jnp.float32)
-            .reshape(mixed, middle)
-            .astype(jnp.bfloat16)
-        )
-        for piece in range(pieces):
-            start = taps + piece * each
-            expand_ref[:, piece * middle : (piece + 1) * middle] = (
-                weights_ref[:, start : start + each, :]
-                .astype(jnp.float32)
-                .reshape(shards_of * each, middle)
-                .astype(jnp.bfloat16)
-            )
         edge = jnp.zeros((images, middle), jnp.bfloat16)
         first_ref[0] = jnp.zeros((wide, middle), jnp.bfloat16)
         first_ref[side + 1] = jnp.zeros((wide, middle), jnp.bfloat16)
@@ -242,6 +311,24 @@
             return carry
 
         lax.fori_loop(0, side, norm, 0)
+        for half in halves:
+            half.wait()
+        for half in range(2):
+            weight_ref[:, half * lane : (half + 1) * lane] = (
+                halves_ref[half, :, :taps, :]
+                .astype(jnp.float32)
+                .reshape(mixed, lane)
+                .astype(jnp.bfloat16)
+            )
+            for piece in range(pieces):
+                start = taps + piece * each
+                column = (half * pieces + piece) * lane
+                expand_ref[:, column : column + lane] = (
+                    halves_ref[half, :, start : start + each, :]
+                    .astype(jnp.float32)
+                    .reshape(shards_of * each, lane)
+                    .astype(jnp.bfloat16)
+                )
 
         def one(step, carry):
             total, squares = carry
@@ -269,24 +356,26 @@
     return pl.pallas_call(
         body,
         name="spatial_stage",
-        in_specs=[HBM] + [VM] * 4,
+        in_specs=[SM] + [HBM] * 3 + [VM] * 3,
         out_specs=[VM] * 5,
         out_shape=[
             jax.ShapeDtypeStruct((rows, middle), jnp.float32),
             jax.ShapeDtypeStruct((2, middle), jnp.float32),
             jax.ShapeDtypeStruct((1, middle), jnp.float32),
             jax.ShapeDtypeStruct((1, middle), jnp.float32),
-            jax.ShapeDtypeStruct((shards_of * each, pieces * middle), jnp.bfloat16),
+            jax.ShapeDtypeStruct((shards_of * each, 2 * pieces * lane), jnp.bfloat16),
         ],
         scratch_shapes=[
             pltpu.VMEM((side + 2, wide, middle), jnp.bfloat16),
             pltpu.VMEM((mixed, middle), jnp.bfloat16),
             pltpu.VMEM((rows, middle), jnp.float32),
+            pltpu.VMEM((2, shards_of, packed, lane), jnp.bfloat16),
             pltpu.SemaphoreType.DMA((side,)),
+            pltpu.SemaphoreType.DMA((2,)),
         ],
         compiler_params=pltpu.CompilerParams(vmem_limit_bytes=24 << 20),
         cost_estimate=cost(2 * rows * mixed * middle),
-    )(reduced, sums, gain, bias, weights)
+    )(own, *in_hbm(reduced, mine, other), sums, gain, bias)
 
 
 def second_stage(spatial, sums, gain, bias, weight, side, images, row_count):
@@ -410,15 +499,41 @@
     )(second, maps, sums, gain, bias, weight)
 
 
-def probe_stage(pooled, class_w, shift, labels, image_count):
+def probe_stage(own, pooled, mine, other, first_row, shift, labels, image_count):
     images, channels = pooled.shape
-    lanes = class_w.shape[1]
-
-    def body(labels_ref, pooled_ref, class_ref, shift_ref, margin_ref):
-        logits = (
-            jnp.dot(pooled_ref[...], class_ref[...], preferred_element_type=jnp.float32)
-            + shift_ref[...]
+    lanes = shift.shape[1]
+    shards_of, packed, lane = mine.shape
+    class_rows = packed - first_row
+    cols = channels // shards_of
+    tiles = class_rows // cols
+
+    def body(own_ref, labels_ref, pooled_ref, mine_ref, other_ref, shift_ref, margin_ref,
+             halves_ref, sems):
+        core = own_ref[1]
+        rows_of = pl.ds(first_row, class_rows)
+        fetch(
+            [
+                (mine_ref.at[:, rows_of, :], halves_ref.at[core]),
+                (other_ref.at[:, rows_of, :], halves_ref.at[1 - core]),
+            ],
+            sems,
         )
+        parts = []
+        for half in range(2):
+            for pair in range(tiles // 2):
+                kernel = jnp.concatenate(
+                    [
+                        halves_ref[half, :, tile * cols : (tile + 1) * cols, :].reshape(
+                            channels, lane
+                        )
+                        for tile in (2 * pair, 2 * pair + 1)
+                    ],
+                    axis=1,
+                )
+                parts.append(
+                    jnp.dot(pooled_ref[...], kernel, preferred_element_type=jnp.float32)
+                )
+        logits = jnp.concatenate(parts, axis=1) + shift_ref[...]
         index = lax.broadcasted_iota(jnp.int32, (images, 1), 0)
         column = jnp.zeros((images, 1), jnp.int32)
         for image in range(images):
@@ -432,11 +547,15 @@
     return pl.pallas_call(
         body,
         name="probe_stage",
-        in_specs=[SM, VM, VM, VM],
+        in_specs=[SM, SM, VM, HBM, HBM, VM],
         out_specs=VM,
         out_shape=jax.ShapeDtypeStruct((1, 128), jnp.float32),
-        compiler_params=pltpu.CompilerParams(vmem_limit_bytes=8 << 20),
-    )(labels, pooled, class_w, shift)
+        scratch_shapes=[
+            pltpu.VMEM((2, shards_of, class_rows, lane), jnp.bfloat16),
+            pltpu.SemaphoreType.DMA((2,)),
+        ],
+        compiler_params=pltpu.CompilerParams(vmem_limit_bytes=12 << 20),
+    )(own, labels, pooled, *in_hbm(mine, other), shift)
 
 
 def shards(activations, labels, t_values, point_index, w_reduce, w_spatial, w_expand, w_classes,
@@ -446,26 +565,27 @@
     image_count = images * lax.axis_size(BATCH)
     row_count = float(image_count * side * side)
     lanes = -(-class_bias.shape[1] // 128) * 128
-    own = jnp.reshape(lax.axis_index(POINT), (1,)).astype(jnp.int32)
+    own = jnp.stack([lax.axis_index(POINT), lax.axis_index("core")]).astype(jnp.int32)
     sent, gain, bias, shift = first_weights(
         t_values, point_index, own, w_reduce, norm_gain, norm_bias, class_bias, lanes
     )
     reduce_w = exchange(sent).reshape(channels, middle)
-    packed, class_sent = other_weights(
-        t_values, point_index, w_spatial, w_expand, jnp.swapaxes(w_classes, 1, 2), lanes
+    packed = other_weights(
+        t_values, point_index, own, w_spatial, w_expand, jnp.swapaxes(w_classes, 1, 2), lanes
     )
     packed, reduce_w = lax.optimization_barrier((packed, reduce_w))
-    weights = exchange(packed)
+    mine = exchange(packed)
     maps = jnp.transpose(activations, (1, 2, 0, 3)).reshape(side * side * images, channels)
     maps = pltpu.with_memory_space_constraint(maps, pltpu.HBM)
     reduced, sums = reduce_stage(maps, reduce_w, side, images)
-    class_sent, sums = lax.optimization_barrier((class_sent, sums))
-    class_w = exchange(class_sent).reshape(channels, lanes)
     sums = batch_sum(sums)
-    reduced = pltpu.with_memory_space_constraint(reduced, pltpu.HBM)
+    mine, sums = lax.optimization_barrier((mine, sums))
+    other = lax.ppermute(mine, "core", [(0, 1), (1, 0)])
+    taps = w_spatial.shape[1]
+    expand_rows = w_expand.shape[1]
     spatial, sums, mean_one, var_one, expand_w = spatial_stage(
-        reduced, sums, gain[:, :middle], bias[:, :middle], weights, w_spatial.shape[1], side,
-        images, row_count
+        own, reduced, sums, gain[:, :middle], bias[:, :middle], mine, other, taps, expand_rows,
+        side, images, row_count
     )
     sums = batch_sum(sums)
     second, sums, mean_two, var_two = second_stage(
@@ -477,7 +597,9 @@
         second, maps, sums, gain[:, 2 * middle :], bias[:, 2 * middle :], expand_w, side, images,
         row_count
     )
-    margin = probe_stage(pooled, class_w, shift, labels, image_count)
+    margin = probe_stage(
+        own, pooled, mine, other, taps + 4 * expand_rows, shift, labels, image_count
+    )
     margin = batch_sum(margin)
     points = lax.axis_size(POINT)
     copies = jnp.broadcast_to(margin[None], (points, 1, 128))

time: 155 us -> 124 us (0.80)
  blocking collectives: 37.1 us -> 15.2 us
  local copies, waits for them, and re-layouts: 14.3 us -> 2.15 us
  starting transfers between devices: 26.1 us -> 19.4 us
  Pallas kernels: 39.9 us -> 45.2 us
  waiting for transfers between devices: 36 us -> 40.9 us
    all_to_all x1, blocking collectives: 37.1 us -> 15.2 us  [exchange(): return lax.all_to_all(x, POINT, split_axis=0, concat_axis=0, tiled=True)]
    unnamed x32 -> x6, local copies, waits for them, and re-layouts: 13.5 us -> 1.3 us
    all_to_all x3 -> x2, starting transfers between devices: 21.7 us -> 14.9 us  [exchange(): return lax.all_to_all(x, POINT, split_axis=0, concat_axis=0, tiled=True)]
    pallas_call x4, Pallas kernels: 18.3 us -> 23.5 us  [the longest x1 14.4 us: spatial_stage(): pl.pallas_call(body, name='spatial_stage', in_specs=[SM] + [HBM] * 3 + [V...]
    ppermute x0 -> x1, waiting for transfers between devices: none -> 3.87 us  [shards(): other = lax.ppermute(mine, 'core', [(0, 1), (1, 0)])]
    all_to_all x3 -> x2, waiting for transfers between devices: 20.8 us -> 22 us  [exchange(): return lax.all_to_all(x, POINT, split_axis=0, concat_axis=0, tiled=True)]
  transfers between devices with their start and end apart: 11 -> 11, of which waited for: 10 -> 11; matrix products, arithmetic and copies ran while one was open for 0% -> 0% of each run, Pallas kernels for 24% -> 9%
where the time goes in v2:
time: 124 us
  Pallas kernels  45.2 us (36%)
  waiting for transfers between devices  40.9 us (33%)
  starting transfers between devices  19.4 us (16%)
  blocking collectives  15.2 us (12%)
  local copies, waits for them, and re-layouts  2.15 us (2%)
    all_to_all x2, waiting for transfers between devices, exchange(): return lax.all_to_all(x, POINT, split_axis=0, concat_axis=0, tiled=True)  22 us
    all_to_all x1, blocking collectives, exchange(): return lax.all_to_all(x, POINT, split_axis=0, concat_axis=0, tiled=True)  15.2 us
    all_to_all x2, starting transfers between devices, exchange(): return lax.all_to_all(x, POINT, split_axis=0, concat_axis=0, tiled=True)  14.9 us
    pallas_call x1, Pallas kernels, spatial_stage(): pl.pallas_call(body, name='spatial_stage', in_specs=[SM] + [HBM] * 3 + [V...  14.4 us
    ppermute x4, waiting for transfers between devices, batch_sum(): return x + lax.ppermute(x, 'bz', [(0, 1), (1, 0)])  10.5 us
    pallas_call x1, Pallas kernels, output_stage(): pl.pallas_call(body, name='output_stage', in_specs=[VM, HBM] + [VM] * 4,...  8.57 us
    pallas_call x1, Pallas kernels, reduce_stage(): pl.pallas_call(body, name='reduce_stage', in_specs=[HBM, VM], out_specs=[...  7.96 us
    pallas_call x1, Pallas kernels, second_stage(): pl.pallas_call(body, name='second_stage', in_specs=[VM] * 5, out_specs=[V...  5.2 us
  transfers between devices with their start and end apart: 11, of which 11 were waited for; matrix products, arithmetic and copies ran while one was open for 0% of the time, Pallas kernels for 9%

profile of v2, /device:TPU:0, one launch (start us, length us, event | category | flops | bytes accessed | tf_op | source)
XLA Modules:
  0.0 123.8 jit_solution(4033450791176908083)
XLA Ops:
  0.6 0.1 pad_add_fusion.own_ref
  0.7 2.8 %first_weights.1 = (bf16[32,32,256]{2,1,0:T(8,128)(2,1)}, f32[1,1536]{1,0:T(1,128)S(1)}, f32[1,1536]{1,0:T(1,128)S(1)}, f32[1,1024]{1,0:T(1,128)S(1)}) custom-call(s32[2]{0:T(128)S(1)} %pad_add_fusion.own_ref, f32[64]{0:T(128)} %refs_0_.1, s32[32]{0:T(128)} %refs_1_.1, bf16[3,32,256]{2,1,0:T(8,128)(2,1)} %refs_2_.1, f32[3,1536]{1,0:T(4,128)} %refs_3_.1, ...), custom_call_target="tpu_custom_call" | custom-call | tf_op jit(solution)/shard_map/first_weights/pallas_call | solution.py:74
  3.5 10.8 %all-to-all-start = ((bf16[32,32,256]{2,1,0:T(8,128)(2,1)}), bf16[32,32,256]{2,1,0:T(8,128)(2,1)S(1)}, u32[]{:S(2)}, u32[]{:S(2)}) async-start(bf16[32,32,256]{2,1,0:T(8,128)(2,1)} %get-tuple-element.29), calls=%async_computation | async-start | bytes 1048576 | tf_op jit(solution)/shard_map/all_to_all | solution.py:183
  14.3 3.6 %other_weights.1 = bf16[32,232,128]{2,1,0:T(8,128)(2,1)} custom-call(s32[2]{0:T(128)S(1)} %pad_add_fusion.own_ref, f32[64]{0:T(128)} %refs_0_.1, s32[32]{0:T(128)} %refs_1_.1, bf16[3,72,256]{2,1,0:T(8,128)(2,1)} %spatial_in.1, bf16[3,8,1024]{2,1,0:T(8,128)(2,1)} %expand_in.1, bf16[3,32,1000]{2,1,0:T(8,128)(2,1)} %bitcast.12), custom_call_target="tpu_custom_call" | custom-call | tf_op jit(solution)/shard_map/other_weights/pallas_call | solution.py:160
  17.9 9.5 %all-to-all-done = bf16[32,32,256]{2,1,0:T(8,128)(2,1)S(1)} async-done(((bf16[32,32,256]{2,1,0:T(8,128)(2,1)}), bf16[32,32,256]{2,1,0:T(8,128)(2,1)S(1)}, u32[]{:S(2)}, u32[]{:S(2)}) %all-to-all-start) | async-done | bytes 524320 | tf_op jit(solution)/shard_map/all_to_all | solution.py:183
  27.4 4.1 %all-to-all-start.1 = ((bf16[32,232,128]{2,1,0:T(8,128)(2,1)}), bf16[32,232,128]{2,1,0:T(8,128)(2,1)S(1)}, u32[]{:S(2)}, u32[]{:S(2)}) async-start(bf16[32,232,128]{2,1,0:T(8,128)(2,1)} %other_weights.1), calls=%async_computation.1 | async-start | bytes 3801088 | tf_op jit(solution)/shard_map/all_to_all | solution.py:183
  31.5 8.0 %reduce_stage.1 = (f32[6272,256]{1,0:T(8,128)}, f32[2,256]{1,0:T(2,128)S(1)}) custom-call(bf16[6272,1024]{1,0:T(8,128)(2,1)} %bitcast.10, bf16[1024,256]{1,0:T(8,128)(2,1)S(1)} %bitcast.9), custom_call_target="tpu_custom_call" | custom-call | flops 3288334336 | bytes 6422528 | tf_op jit(solution)/shard_map/reduce_stage/pallas_call | solution.py:242
  39.5 0.1 collective-permute-start
  39.6 1.1 collective-permute-done
  40.7 1.0 collective-permute-start.1
  41.8 2.7 %collective-permute-done.1 = f32[2,256]{1,0:T(2,128)S(1)} collective-permute-done((f32[2,256]{1,0:T(2,128)S(1)}, f32[2,256]{1,0:T(2,128)S(1)}, u32[]{:S(2)}, u32[]{:S(2)}) %collective-permute-start.1) | collective-permute-done | bytes 2080 | tf_op jit(solution)/shard_map/ppermute | solution.py:188
  44.5 12.6 %all-to-all-done.1.mine_ref = bf16[32,232,128]{2,1,0:T(8,128)(2,1)S(1)} async-done(((bf16[32,232,128]{2,1,0:T(8,128)(2,1)}), bf16[32,232,128]{2,1,0:T(8,128)(2,1)S(1)}, u32[]{:S(2)}, u32[]{:S(2)}) %all-to-all-start.1) | async-done | bytes 1900576 | tf_op jit(solution)/shard_map/all_to_all | solution.py:183
  57.1 0.0 copy-start.1
  57.1 0.0 collective-permute-start.2
  57.1 3.9 %collective-permute-done.2.other_ref = bf16[32,232,128]{2,1,0:T(8,128)(2,1)S(1)} collective-permute-done((bf16[32,232,128]{2,1,0:T(8,128)(2,1)S(1)}, bf16[32,232,128]{2,1,0:T(8,128)(2,1)S(1)}, u32[]{:S(2)}, u32[]{:S(2)}) %collective-permute-start.2) | collective-permute-done | bytes 1900576 | tf_op jit(solution)/shard_map/ppermute | solution.py:583
  60.9 0.0 copy-start.2
  60.9 0.0 copy-done.1
  60.9 1.3 %copy-done.2 = bf16[32,232,128]{2,1,0:T(8,128)(2,1)} copy-done((bf16[32,232,128]{2,1,0:T(8,128)(2,1)}, bf16[32,232,128]{2,1,0:T(8,128)(2,1)S(1)}, u32[]{:S(2)}) %copy-start.2) | copy-done | bytes 1900568
  62.2 14.4 %spatial_stage.1 = (f32[6272,256]{1,0:T(8,128)S(1)}, f32[2,256]{1,0:T(2,128)S(1)}, f32[1,256]{1,0:T(1,128)}, f32[1,256]{1,0:T(1,128)}, bf16[256,1024]{1,0:T(8,128)(2,1)S(1)}) custom-call(s32[2]{0:T(128)S(1)} %pad_add_fusion.own_ref, f32[6272,256]{1,0:T(8,128)} %get-tuple-element.31.reduced_ref, bf16[32,232,128]{2,1,0:T(8,128)(2,1)} %copy-done.1, ...), custom_call_target="tpu_custom_call" | custom-call | flops 7398752256 | bytes 14450688 | tf_op jit(solution)/shard_map/spatial_stage/pallas_call | solution.py:356
  76.6 0.2 collective-permute-start.3
  76.8 1.0 collective-permute-done.3
  77.9 1.0 collective-permute-start.4
  78.9 2.6 %collective-permute-done.4 = f32[2,256]{1,0:T(2,128)S(1)} collective-permute-done((f32[2,256]{1,0:T(2,128)S(1)}, f32[2,256]{1,0:T(2,128)S(1)}, u32[]{:S(2)}, u32[]{:S(2)}) %collective-permute-start.4) | collective-permute-done | bytes 2080 | tf_op jit(solution)/shard_map/ppermute | solution.py:188
  81.5 5.2 %second_stage.1 = (bf16[6272,256]{1,0:T(8,128)(2,1)S(1)}, f32[2,1024]{1,0:T(2,128)S(1)}, f32[1,256]{1,0:T(1,128)}, f32[1,256]{1,0:T(1,128)}) custom-call(f32[6272,256]{1,0:T(8,128)S(1)} %get-tuple-element.40.spatial_ref, f32[2,256]{1,0:T(2,128)S(1)} %add.35.sums_ref, f32[1,256]{1,0:T(1,128)S(1)} %get-tuple-element.56.gain_ref, ...), custom_call_target="tpu_custom_call" | custom-call | flops 822083584 | bytes 1605632 | tf_op jit(solution)/shard_map/second_stage/pallas_call | solution.py:426
  86.7 0.1 collective-permute-start.5
  86.8 1.2 collective-permute-done.5
  87.9 1.0 collective-permute-start.6
  89.0 2.6 %collective-permute-done.6 = f32[2,1024]{1,0:T(2,128)S(1)} collective-permute-done((f32[2,1024]{1,0:T(2,128)S(1)}, f32[2,1024]{1,0:T(2,128)S(1)}, u32[]{:S(2)}, u32[]{:S(2)}) %collective-permute-start.6) | collective-permute-done | bytes 8224 | tf_op jit(solution)/shard_map/ppermute | solution.py:188
  91.6 0.0 copy-start
  91.6 8.6 %output_stage.1 = (bf16[32,1024]{1,0:T(8,128)(2,1)S(1)}, f32[1,1024]{1,0:T(1,128)}, f32[1,1024]{1,0:T(1,128)}) custom-call(bf16[6272,256]{1,0:T(8,128)(2,1)S(1)} %get-tuple-element.45.second_ref, bf16[6272,1024]{1,0:T(8,128)(2,1)} %bitcast.11, f32[2,1024]{1,0:T(2,128)S(1)} %add.37.sums_ref, f32[1,1024]{1,0:T(1,128)S(1)} %slice.25.gain_ref, ...), custom_call_target="tpu_custom_call" | custom-call | flops 3288334336 | bytes 6422528 | tf_op jit(solution)/shard_map/output_stage/pallas_call | solution.py:482
  100.2 0.0 copy-done
  100.2 2.7 %probe_stage.1 = f32[1,128]{1,0:T(1,128)S(1)} custom-call(s32[2]{0:T(128)S(1)} %pad_add_fusion.own_ref, s32[32]{0:T(128)S(1)} %copy-done, bf16[32,1024]{1,0:T(8,128)(2,1)S(1)} %get-tuple-element.49.pooled_ref, bf16[32,232,128]{2,1,0:T(8,128)(2,1)} %copy-done.1, bf16[32,232,128]{2,1,0:T(8,128)(2,1)} %copy-done.2, f32[1,1024]{1,0:T(1,128)S(1)} %get-tuple-element.50.shift_ref), custom_call_target="tpu_custom_call" | custom-call | tf_op jit(solution)/shard_map/probe_stage/pallas_call | solution.py:547
  102.9 0.1 collective-permute-start.7
  103.0 1.1 collective-permute-done.7
  104.1 1.0 collective-permute-start.8
  105.1 2.5 %collective-permute-done.8 = f32[1,128]{1,0:T(1,128)S(1)} collective-permute-done((f32[1,128]{1,0:T(1,128)S(1)}, f32[1,128]{1,0:T(1,128)S(1)}, u32[]{:S(2)}, u32[]{:S(2)}) %collective-permute-start.8) | collective-permute-done | bytes 544 | tf_op jit(solution)/shard_map/ppermute | solution.py:188
  107.7 15.2 %all_to_all.15 = f32[32,1,128]{2,1,0:T(1,128)S(1)} all-to-all(f32[32,1,128]{2,1,0:T(1,128)S(1)} %broadcast_in_dim.9), channel_id=1, replica_groups=mesh['pz'=2,'px'=4,'py'=4,'bz'=2,'core'=2] {'pz','px','py'}, dimensions={0} | all-to-all | bytes 32768 | tf_op jit(solution)/shard_map/all_to_all | solution.py:183
  122.9 0.8 slice_reduce_fusion
  (12 shorter events, 0.0 us)
Async XLA Ops:
  3.5 23.9 %all-to-all-start = ((bf16[32,32,256]{2,1,0:T(8,128)(2,1)}), bf16[32,32,256]{2,1,0:T(8,128)(2,1)S(1)}, u32[]{:S(2)}, u32[]{:S(2)}) async-start(bf16[32,32,256]{2,1,0:T(8,128)(2,1)} %get-tuple-element.29), calls=%async_computation | async-start | bytes 1048576 | tf_op jit(solution)/shard_map/all_to_all | solution.py:183
  27.4 29.7 %all-to-all-start.1 = ((bf16[32,232,128]{2,1,0:T(8,128)(2,1)}), bf16[32,232,128]{2,1,0:T(8,128)(2,1)S(1)}, u32[]{:S(2)}, u32[]{:S(2)}) async-start(bf16[32,232,128]{2,1,0:T(8,128)(2,1)} %other_weights.1), calls=%async_computation.1 | async-start | bytes 3801088 | tf_op jit(solution)/shard_map/all_to_all | solution.py:183
  39.5 1.2 %collective-permute-start = (f32[2,256]{1,0:T(2,128)S(1)}, f32[2,256]{1,0:T(2,128)S(1)}, u32[]{:S(2)}, u32[]{:S(2)}) collective-permute-start(f32[2,256]{1,0:T(2,128)S(1)} %get-tuple-element.33), channel_id=1, source_target_pairs={{0,1},{1,0},{2,3},{3,2},{4,5},{5,4},{6,7},{7,6},{8,9},{9,8},{10,11... | collective-permute-start | bytes 6152 | tf_op jit(solution)/shard_map/ppermute | solution.py:187
  40.7 3.7 %collective-permute-start.1 = (f32[2,256]{1,0:T(2,128)S(1)}, f32[2,256]{1,0:T(2,128)S(1)}, u32[]{:S(2)}, u32[]{:S(2)}) collective-permute-start(f32[2,256]{1,0:T(2,128)S(1)} %add.32), channel_id=1, source_target_pairs={{0,2},{2,0},{1,3},{3,1},{4,6},{6,4},{5,7},{7,5},{8,10},{10,8},{9,1... | collective-permute-start | bytes 6152 | tf_op jit(solution)/shard_map/ppermute | solution.py:188
  57.1 3.9 %copy-start.1 = (bf16[32,232,128]{2,1,0:T(8,128)(2,1)}, bf16[32,232,128]{2,1,0:T(8,128)(2,1)S(1)}, u32[]{:S(2)}) copy-start(bf16[32,232,128]{2,1,0:T(8,128)(2,1)S(1)} %all-to-all-done.1.mine_ref) | copy-start | bytes 5701636
  57.1 3.9 %collective-permute-start.2 = (bf16[32,232,128]{2,1,0:T(8,128)(2,1)S(1)}, bf16[32,232,128]{2,1,0:T(8,128)(2,1)S(1)}, u32[]{:S(2)}, u32[]{:S(2)}) collective-permute-start(bf16[32,232,128]{2,1,0:T(8,128)(2,1)S(1)} %all-to-all-done.1.mine_ref), channel_id=1, source_target_pairs={{0,1},{1,0},{2,3},{3,2},{4,5},{5,4},{6,7},{7,6},{8,9},{9,8},{10,11... | collective-permute-start | bytes 5701640 | tf_op jit(solution)/shard_map/ppermute | solution.py:583
  60.9 1.3 %copy-start.2 = (bf16[32,232,128]{2,1,0:T(8,128)(2,1)}, bf16[32,232,128]{2,1,0:T(8,128)(2,1)S(1)}, u32[]{:S(2)}) copy-start(bf16[32,232,128]{2,1,0:T(8,128)(2,1)S(1)} %collective-permute-done.2.other_ref) | copy-start | bytes 5701636
  76.6 1.2 %collective-permute-start.3 = (f32[2,256]{1,0:T(2,128)S(1)}, f32[2,256]{1,0:T(2,128)S(1)}, u32[]{:S(2)}, u32[]{:S(2)}) collective-permute-start(f32[2,256]{1,0:T(2,128)S(1)} %get-tuple-element.41), channel_id=1, source_target_pairs={{0,1},{1,0},{2,3},{3,2},{4,5},{5,4},{6,7},{7,6},{8,9},{9,8},{10,11... | collective-permute-start | bytes 6152 | tf_op jit(solution)/shard_map/ppermute | solution.py:187
  77.9 3.6 %collective-permute-start.4 = (f32[2,256]{1,0:T(2,128)S(1)}, f32[2,256]{1,0:T(2,128)S(1)}, u32[]{:S(2)}, u32[]{:S(2)}) collective-permute-start(f32[2,256]{1,0:T(2,128)S(1)} %add.34), channel_id=1, source_target_pairs={{0,2},{2,0},{1,3},{3,1},{4,6},{6,4},{5,7},{7,5},{8,10},{10,8},{9,1... | collective-permute-start | bytes 6152 | tf_op jit(solution)/shard_map/ppermute | solution.py:188
  86.7 1.3 %collective-permute-start.5 = (f32[2,1024]{1,0:T(2,128)S(1)}, f32[2,1024]{1,0:T(2,128)S(1)}, u32[]{:S(2)}, u32[]{:S(2)}) collective-permute-start(f32[2,1024]{1,0:T(2,128)S(1)} %get-tuple-element.46), channel_id=1, source_target_pairs={{0,1},{1,0},{2,3},{3,2},{4,5},{5,4},{6,7},{7,6},{8,9},{9,8},{10,11... | collective-permute-start | bytes 24584 | tf_op jit(solution)/shard_map/ppermute | solution.py:187
  87.9 3.7 %collective-permute-start.6 = (f32[2,1024]{1,0:T(2,128)S(1)}, f32[2,1024]{1,0:T(2,128)S(1)}, u32[]{:S(2)}, u32[]{:S(2)}) collective-permute-start(f32[2,1024]{1,0:T(2,128)S(1)} %add.36), channel_id=1, source_target_pairs={{0,2},{2,0},{1,3},{3,1},{4,6},{6,4},{5,7},{7,5},{8,10},{10,8},{9,1... | collective-permute-start | bytes 24584 | tf_op jit(solution)/shard_map/ppermute | solution.py:188
  91.6 8.6 %copy-start = (s32[32]{0:T(128)S(1)}, s32[32]{0:T(128)}, u32[]{:S(2)}) copy-start(s32[32]{0:T(128)} %labels_ref.1) | copy-start | bytes 388
  102.9 1.2 %collective-permute-start.7 = (f32[1,128]{1,0:T(1,128)S(1)}, f32[1,128]{1,0:T(1,128)S(1)}, u32[]{:S(2)}, u32[]{:S(2)}) collective-permute-start(f32[1,128]{1,0:T(1,128)S(1)} %probe_stage.1), channel_id=1, source_target_pairs={{0,1},{1,0},{2,3},{3,2},{4,5},{5,4},{6,7},{7,6},{8,9},{9,8},{10,11... | collective-permute-start | bytes 1544 | tf_op jit(solution)/shard_map/ppermute | solution.py:187
  104.1 3.6 %collective-permute-start.8 = (f32[1,128]{1,0:T(1,128)S(1)}, f32[1,128]{1,0:T(1,128)S(1)}, u32[]{:S(2)}, u32[]{:S(2)}) collective-permute-start(f32[1,128]{1,0:T(1,128)S(1)} %add.38), channel_id=1, source_target_pairs={{0,2},{2,0},{1,3},{3,1},{4,6},{6,4},{5,7},{7,5},{8,10},{10,8},{9,1... | collective-permute-start | bytes 1544 | tf_op jit(solution)/shard_map/ppermute | solution.py:188

commit v3 on v2

--- a/solution.py
+++ b/solution.py
@@ -9,6 +9,7 @@
 POINT = ("pz", "px", "py")
 BATCH = ("bz", "core")
 EPSILON = 1e-05
+PAIR = 2
 SM = pl.BlockSpec(memory_space=pltpu.SMEM)
 VM = pl.BlockSpec(memory_space=pltpu.VMEM)
 HBM = pl.BlockSpec(memory_space=pltpu.HBM)
@@ -205,7 +206,8 @@
 def reduce_stage(maps, weight, side, images):
     rows, channels = maps.shape
     middle = weight.shape[1]
-    chunk = side * images
+    chunk = PAIR * side * images
+    steps = side // PAIR
 
     def body(maps_ref, weight_ref, reduced_ref, sums_ref, held_ref, block_ref, sems, out_sems):
         def copy(step):
@@ -218,7 +220,7 @@
                 block_ref.at[part], reduced_ref.at[part], out_sems.at[step]
             )
 
-        for step in range(side):
+        for step in range(steps):
             copy(step).start()
 
         def one(step, carry):
@@ -233,10 +235,10 @@
             return total + column_sums(product), squares + column_sums(product * product)
 
         zero = jnp.zeros((8, middle), jnp.float32)
-        total, squares = lax.fori_loop(0, side, one, (zero, zero))
+        total, squares = lax.fori_loop(0, steps, one, (zero, zero))
         sums_ref[0:1, :] = jnp.sum(total, axis=0, keepdims=True)
         sums_ref[1:2, :] = jnp.sum(squares, axis=0, keepdims=True)
-        for step in range(side):
+        for step in range(steps):
             copy_out(step).wait()
 
     return pl.pallas_call(
@@ -251,8 +253,8 @@
         scratch_shapes=[
             pltpu.VMEM((rows, channels), jnp.bfloat16),
             pltpu.VMEM((rows, middle), jnp.float32),
-            pltpu.SemaphoreType.DMA((side,)),
-            pltpu.SemaphoreType.DMA((side,)),
+            pltpu.SemaphoreType.DMA((steps,)),
+            pltpu.SemaphoreType.DMA((steps,)),
         ],
         compiler_params=pltpu.CompilerParams(vmem_limit_bytes=32 << 20),
         cost_estimate=cost(2 * rows * channels * middle),
@@ -272,17 +274,9 @@
 
     def body(own_ref, reduced_ref, mine_ref, other_ref, sums_ref, gain_ref, bias_ref,
              spatial_ref, out_ref, mean_ref, var_ref, expand_ref, first_ref, weight_ref, held_ref,
-             halves_ref, sems, half_sems):
+             halves_ref, sems):
         core = own_ref[1]
-        rows_of = pl.ds(0, packed)
-        halves = [
-            pltpu.make_async_copy(
-                mine_ref.at[:, rows_of, :], halves_ref.at[core], half_sems.at[0]
-            ),
-            pltpu.make_async_copy(
-                other_ref.at[:, rows_of, :], halves_ref.at[1 - core], half_sems.at[1]
-            ),
-        ]
+        low = core == 0
 
         def copy(step):
             part = pl.ds(step * chunk, chunk)
@@ -290,8 +284,6 @@
 
         for step in range(side):
             copy(step).start()
-        for half in halves:
-            half.start()
         mean, var = moments(sums_ref[...], row_count)
         mean_ref[...] = mean
         var_ref[...] = var
@@ -311,11 +303,12 @@
             return carry
 
         lax.fori_loop(0, side, norm, 0)
-        for half in halves:
-            half.wait()
         for half in range(2):
+            first = jnp.where(low, mine_ref[...], other_ref[...])
+            last = jnp.where(low, other_ref[...], mine_ref[...])
+            halves_ref[...] = (first, last)[half]
             weight_ref[:, half * lane : (half + 1) * lane] = (
-                halves_ref[half, :, :taps, :]
+                halves_ref[:, :taps, :]
                 .astype(jnp.float32)
                 .reshape(mixed, lane)
                 .astype(jnp.bfloat16)
@@ -324,7 +317,7 @@
                 start = taps + piece * each
                 column = (half * pieces + piece) * lane
                 expand_ref[:, column : column + lane] = (
-                    halves_ref[half, :, start : start + each, :]
+                    halves_ref[:, start : start + each, :]
                     .astype(jnp.float32)
                     .reshape(shards_of * each, lane)
                     .astype(jnp.bfloat16)
@@ -333,7 +326,9 @@
         def one(step, carry):
             total, squares = carry
             windows = [
-                first_ref[step + dy, dx * images : dx * images + chunk, :]
+                first_ref[
+                    pl.ds(PAIR * step + dy, PAIR), dx * images : dx * images + chunk, :
+                ].reshape(PAIR * chunk, middle)
                 for dy in range(3)
                 for dx in range(3)
             ]
@@ -345,18 +340,18 @@
                 )
                 for tap, window in enumerate(windows)
             )
-            spatial_ref[pl.ds(step * chunk, chunk), :] = product
+            spatial_ref[pl.ds(step * PAIR * chunk, PAIR * chunk), :] = product
             return total + column_sums(product), squares + column_sums(product * product)
 
         zero = jnp.zeros((8, middle), jnp.float32)
-        total, squares = lax.fori_loop(0, side, one, (zero, zero))
+        total, squares = lax.fori_loop(0, side // PAIR, one, (zero, zero))
         out_ref[0:1, :] = jnp.sum(total, axis=0, keepdims=True)
         out_ref[1:2, :] = jnp.sum(squares, axis=0, keepdims=True)
 
     return pl.pallas_call(
         body,
         name="spatial_stage",
-        in_specs=[SM] + [HBM] * 3 + [VM] * 3,
+        in_specs=[SM, HBM] + [VM] * 5,
         out_specs=[VM] * 5,
         out_shape=[
             jax.ShapeDtypeStruct((rows, middle), jnp.float32),
@@ -369,19 +364,18 @@
             pltpu.VMEM((side + 2, wide, middle), jnp.bfloat16),
             pltpu.VMEM((mixed, middle), jnp.bfloat16),
             pltpu.VMEM((rows, middle), jnp.float32),
-            pltpu.VMEM((2, shards_of, packed, lane), jnp.bfloat16),
+            pltpu.VMEM((shards_of, packed, lane), jnp.bfloat16),
             pltpu.SemaphoreType.DMA((side,)),
-            pltpu.SemaphoreType.DMA((2,)),
         ],
         compiler_params=pltpu.CompilerParams(vmem_limit_bytes=24 << 20),
         cost_estimate=cost(2 * rows * mixed * middle),
-    )(own, *in_hbm(reduced, mine, other), sums, gain, bias)
+    )(own, *in_hbm(reduced), mine, other, sums, gain, bias)
 
 
 def second_stage(spatial, sums, gain, bias, weight, side, images, row_count):
     rows, middle = spatial.shape
     channels = weight.shape[1]
-    chunk = side * images
+    chunk = PAIR * side * images
 
     def body(spatial_ref, sums_ref, gain_ref, bias_ref, weight_ref, second_ref, out_ref,
              mean_ref, var_ref):
@@ -403,7 +397,7 @@
 
         total, gram = lax.fori_loop(
             0,
-            side,
+            side // PAIR,
             one,
             (jnp.zeros((8, middle), jnp.float32), jnp.zeros((middle, middle), jnp.float32)),
         )
@@ -499,33 +493,25 @@
     )(second, maps, sums, gain, bias, weight)
 
 
-def probe_stage(own, pooled, mine, other, first_row, shift, labels, image_count):
+def probe_stage(own, pooled, mine, other, shift, labels, image_count):
     images, channels = pooled.shape
     lanes = shift.shape[1]
-    shards_of, packed, lane = mine.shape
-    class_rows = packed - first_row
+    shards_of, class_rows, lane = mine.shape
     cols = channels // shards_of
     tiles = class_rows // cols
 
-    def body(own_ref, labels_ref, pooled_ref, mine_ref, other_ref, shift_ref, margin_ref,
-             halves_ref, sems):
-        core = own_ref[1]
-        rows_of = pl.ds(first_row, class_rows)
-        fetch(
-            [
-                (mine_ref.at[:, rows_of, :], halves_ref.at[core]),
-                (other_ref.at[:, rows_of, :], halves_ref.at[1 - core]),
-            ],
-            sems,
-        )
+    def body(own_ref, labels_ref, pooled_ref, mine_ref, other_ref, shift_ref, margin_ref):
+        low = own_ref[1] == 0
         parts = []
         for half in range(2):
             for pair in range(tiles // 2):
                 kernel = jnp.concatenate(
                     [
-                        halves_ref[half, :, tile * cols : (tile + 1) * cols, :].reshape(
-                            channels, lane
-                        )
+                        jnp.where(
+                            low,
+                            (mine_ref, other_ref)[half][:, tile * cols : (tile + 1) * cols, :],
+                            (other_ref, mine_ref)[half][:, tile * cols : (tile + 1) * cols, :],
+                        ).reshape(channels, lane)
                         for tile in (2 * pair, 2 * pair + 1)
                     ],
                     axis=1,
@@ -547,15 +533,11 @@
     return pl.pallas_call(
         body,
         name="probe_stage",
-        in_specs=[SM, SM, VM, HBM, HBM, VM],
+        in_specs=[SM, SM, VM, VM, VM, VM],
         out_specs=VM,
         out_shape=jax.ShapeDtypeStruct((1, 128), jnp.float32),
-        scratch_shapes=[
-            pltpu.VMEM((2, shards_of, class_rows, lane), jnp.bfloat16),
-            pltpu.SemaphoreType.DMA((2,)),
-        ],
         compiler_params=pltpu.CompilerParams(vmem_limit_bytes=12 << 20),
-    )(own, labels, pooled, *in_hbm(mine, other), shift)
+    )(own, labels, pooled, mine, other, shift)
 
 
 def shards(activations, labels, t_values, point_index, w_reduce, w_spatial, w_expand, w_classes,
@@ -580,9 +562,14 @@
     reduced, sums = reduce_stage(maps, reduce_w, side, images)
     sums = batch_sum(sums)
     mine, sums = lax.optimization_barrier((mine, sums))
-    other = lax.ppermute(mine, "core", [(0, 1), (1, 0)])
     taps = w_spatial.shape[1]
     expand_rows = w_expand.shape[1]
+    conv_rows = taps + channels // middle * expand_rows
+    swap = [(0, 1), (1, 0)]
+    mine, class_mine = mine[:, :conv_rows], mine[:, conv_rows:]
+    other = lax.ppermute(mine, "core", swap)
+    class_mine, other = lax.optimization_barrier((class_mine, other))
+    class_other = lax.ppermute(class_mine, "core", swap)
     spatial, sums, mean_one, var_one, expand_w = spatial_stage(
         own, reduced, sums, gain[:, :middle], bias[:, :middle], mine, other, taps, expand_rows,
         side, images, row_count
@@ -598,7 +585,7 @@
         row_count
     )
     margin = probe_stage(
-        own, pooled, mine, other, taps + 4 * expand_rows, shift, labels, image_count
+        own, pooled, class_mine, class_other, shift, labels, image_count
     )
     margin = batch_sum(margin)
     points = lax.axis_size(POINT)

time: 124 us -> 117 us (0.944)
  Pallas kernels: 45.2 us -> 40.7 us
  waiting for transfers between devices: 40.9 us -> 39.1 us
    pallas_call x2, Pallas kernels: 17.1 us -> 14.3 us  [the longest x1 13.1 us: spatial_stage(): pl.pallas_call(body, name='spatial_stage', in_specs=[SM, HBM] + [VM] * 5,...]
    ppermute x1 -> x2, waiting for transfers between devices: 3.87 us -> 2.23 us  [the longest x1 2.23 us: shards(): other = lax.ppermute(mine, 'core', swap)]
    pallas_call x1, Pallas kernels: 5.2 us -> 3.58 us  [second_stage(): pl.pallas_call(body, name='second_stage', in_specs=[VM] * 5, out_specs=[V...]
    unnamed x6 -> x2, local copies, waits for them, and re-layouts: 1.3 us -> 0.01 us
  transfers between devices with their start and end apart: 11 -> 12, of which waited for: 11 -> 11; matrix products, arithmetic and copies ran while one was open for 0% -> 0% of each run, Pallas kernels for 9% -> 31%
where the time goes in v3:
time: 117 us
  Pallas kernels  40.7 us (35%)
  waiting for transfers between devices  39.1 us (33%)
  starting transfers between devices  19.9 us (17%)
  blocking collectives  15.2 us (13%)
    all_to_all x2, waiting for transfers between devices, exchange(): return lax.all_to_all(x, POINT, split_axis=0, concat_axis=0, tiled=True)  22.1 us
    all_to_all x1, blocking collectives, exchange(): return lax.all_to_all(x, POINT, split_axis=0, concat_axis=0, tiled=True)  15.2 us
    all_to_all x2, starting transfers between devices, exchange(): return lax.all_to_all(x, POINT, split_axis=0, concat_axis=0, tiled=True)  14.9 us
    pallas_call x1, Pallas kernels, spatial_stage(): pl.pallas_call(body, name='spatial_stage', in_specs=[SM, HBM] + [VM] * 5,...  13.1 us
    ppermute x4, waiting for transfers between devices, batch_sum(): return x + lax.ppermute(x, 'bz', [(0, 1), (1, 0)])  10.5 us
    pallas_call x1, Pallas kernels, output_stage(): pl.pallas_call(body, name='output_stage', in_specs=[VM, HBM] + [VM] * 4,...  8.57 us
    pallas_call x1, Pallas kernels, reduce_stage(): pl.pallas_call(body, name='reduce_stage', in_specs=[HBM, VM], out_specs=[...  7.91 us
    ppermute x4, waiting for transfers between devices, batch_sum(): x = x + lax.ppermute(x, 'core', [(0, 1), (1, 0)])  4.28 us
  transfers between devices with their start and end apart: 12, of which 11 were waited for; matrix products, arithmetic and copies ran while one was open for 0% of the time, Pallas kernels for 31%

profile of v3, /device:TPU:0, one launch (start us, length us, event | category | flops | bytes accessed | tf_op | source)
XLA Modules:
  0.0 116.8 jit_solution(12247413108494844014)
XLA Ops:
  0.6 0.1 pad_add_fusion.own_ref
  0.7 2.8 %first_weights.1 = (bf16[32,32,256]{2,1,0:T(8,128)(2,1)}, f32[1,1536]{1,0:T(1,128)S(1)}, f32[1,1536]{1,0:T(1,128)S(1)}, f32[1,1024]{1,0:T(1,128)S(1)}) custom-call(s32[2]{0:T(128)S(1)} %pad_add_fusion.own_ref, f32[64]{0:T(128)} %refs_0_.1, s32[32]{0:T(128)} %refs_1_.1, bf16[3,32,256]{2,1,0:T(8,128)(2,1)} %refs_2_.1, f32[3,1536]{1,0:T(4,128)} %refs_3_.1, ...), custom_call_target="tpu_custom_call" | custom-call | tf_op jit(solution)/shard_map/first_weights/pallas_call | solution.py:75
  3.5 10.8 %all-to-all-start = ((bf16[32,32,256]{2,1,0:T(8,128)(2,1)}), bf16[32,32,256]{2,1,0:T(8,128)(2,1)S(1)}, u32[]{:S(2)}, u32[]{:S(2)}) async-start(bf16[32,32,256]{2,1,0:T(8,128)(2,1)} %get-tuple-element.31), calls=%async_computation | async-start | bytes 1048576 | tf_op jit(solution)/shard_map/all_to_all | solution.py:184
  14.3 3.6 %other_weights.1 = bf16[32,232,128]{2,1,0:T(8,128)(2,1)} custom-call(s32[2]{0:T(128)S(1)} %pad_add_fusion.own_ref, f32[64]{0:T(128)} %refs_0_.1, s32[32]{0:T(128)} %refs_1_.1, bf16[3,72,256]{2,1,0:T(8,128)(2,1)} %spatial_in.1, bf16[3,8,1024]{2,1,0:T(8,128)(2,1)} %expand_in.1, bf16[3,32,1000]{2,1,0:T(8,128)(2,1)} %bitcast.12), custom_call_target="tpu_custom_call" | custom-call | tf_op jit(solution)/shard_map/other_weights/pallas_call | solution.py:161
  17.9 9.5 %all-to-all-done = bf16[32,32,256]{2,1,0:T(8,128)(2,1)S(1)} async-done(((bf16[32,32,256]{2,1,0:T(8,128)(2,1)}), bf16[32,32,256]{2,1,0:T(8,128)(2,1)S(1)}, u32[]{:S(2)}, u32[]{:S(2)}) %all-to-all-start) | async-done | bytes 524320 | tf_op jit(solution)/shard_map/all_to_all | solution.py:184
  27.4 4.1 %all-to-all-start.1 = ((bf16[32,232,128]{2,1,0:T(8,128)(2,1)}), bf16[32,232,128]{2,1,0:T(8,128)(2,1)S(1)}, u32[]{:S(2)}, u32[]{:S(2)}) async-start(bf16[32,232,128]{2,1,0:T(8,128)(2,1)} %other_weights.1), calls=%async_computation.1 | async-start | bytes 3801088 | tf_op jit(solution)/shard_map/all_to_all | solution.py:184
  31.5 7.9 %reduce_stage.1 = (f32[6272,256]{1,0:T(8,128)}, f32[2,256]{1,0:T(2,128)S(1)}) custom-call(bf16[6272,1024]{1,0:T(8,128)(2,1)} %bitcast.10, bf16[1024,256]{1,0:T(8,128)(2,1)S(1)} %bitcast.9), custom_call_target="tpu_custom_call" | custom-call | flops 3288334336 | bytes 6422528 | tf_op jit(solution)/shard_map/reduce_stage/pallas_call | solution.py:244
  39.5 0.1 collective-permute-start
  39.6 1.1 collective-permute-done
  40.7 1.0 collective-permute-start.1
  41.7 2.7 %collective-permute-done.1 = f32[2,256]{1,0:T(2,128)S(1)} collective-permute-done((f32[2,256]{1,0:T(2,128)S(1)}, f32[2,256]{1,0:T(2,128)S(1)}, u32[]{:S(2)}, u32[]{:S(2)}) %collective-permute-start.1) | collective-permute-done | bytes 2080 | tf_op jit(solution)/shard_map/ppermute | solution.py:189
  44.4 12.6 %all-to-all-done.1 = bf16[32,232,128]{2,1,0:T(8,128)(2,1)S(1)} async-done(((bf16[32,232,128]{2,1,0:T(8,128)(2,1)}), bf16[32,232,128]{2,1,0:T(8,128)(2,1)S(1)}, u32[]{:S(2)}, u32[]{:S(2)}) %all-to-all-start.1) | async-done | bytes 1900576 | tf_op jit(solution)/shard_map/all_to_all | solution.py:184
  57.1 0.1 slice.27.mine_ref
  57.1 0.1 collective-permute-start.2
  57.2 0.1 slice.28.mine_ref
  57.4 2.2 %collective-permute-done.2.other_ref = bf16[32,104,128]{2,1,0:T(8,128)(2,1)S(1)} collective-permute-done((bf16[32,104,128]{2,1,0:T(8,128)(2,1)S(1)}, bf16[32,104,128]{2,1,0:T(8,128)(2,1)S(1)}, u32[]{:S(2)}, u32[]{:S(2)}) %collective-permute-start.2) | collective-permute-done | bytes 852000 | tf_op jit(solution)/shard_map/ppermute | solution.py:570
  59.6 0.1 collective-permute-start.7
  59.7 13.1 %spatial_stage.1 = (f32[6272,256]{1,0:T(8,128)S(1)}, f32[2,256]{1,0:T(2,128)S(1)}, f32[1,256]{1,0:T(1,128)}, f32[1,256]{1,0:T(1,128)}, bf16[256,1024]{1,0:T(8,128)(2,1)S(1)}) custom-call(s32[2]{0:T(128)S(1)} %pad_add_fusion.own_ref, f32[6272,256]{1,0:T(8,128)} %get-tuple-element.33.reduced_ref, bf16[32,104,128]{2,1,0:T(8,128)(2,1)S(1)} %slice.27.mine_ref, ...), custom_call_target="tpu_custom_call" | custom-call | flops 7398752256 | bytes 14450688 | tf_op jit(solution)/shard_map/spatial_stage/pallas_call | solution.py:351
  72.8 0.5 collective-permute-start.3
  73.3 0.8 collective-permute-done.3
  74.1 1.0 collective-permute-start.4
  75.1 2.6 %collective-permute-done.4 = f32[2,256]{1,0:T(2,128)S(1)} collective-permute-done((f32[2,256]{1,0:T(2,128)S(1)}, f32[2,256]{1,0:T(2,128)S(1)}, u32[]{:S(2)}, u32[]{:S(2)}) %collective-permute-start.4) | collective-permute-done | bytes 2080 | tf_op jit(solution)/shard_map/ppermute | solution.py:189
  77.7 3.6 %second_stage.1 = (bf16[6272,256]{1,0:T(8,128)(2,1)S(1)}, f32[2,1024]{1,0:T(2,128)S(1)}, f32[1,256]{1,0:T(1,128)}, f32[1,256]{1,0:T(1,128)}) custom-call(f32[6272,256]{1,0:T(8,128)S(1)} %get-tuple-element.43.spatial_ref, f32[2,256]{1,0:T(2,128)S(1)} %add.35.sums_ref, f32[1,256]{1,0:T(1,128)S(1)} %get-tuple-element.60.gain_ref, ...), custom_call_target="tpu_custom_call" | custom-call | flops 822083584 | bytes 1605632 | tf_op jit(solution)/shard_map/second_stage/pallas_call | solution.py:420
  81.3 0.1 collective-permute-start.5
  81.3 1.2 collective-permute-done.5
  82.5 1.0 collective-permute-start.6
  83.5 2.6 %collective-permute-done.6 = f32[2,1024]{1,0:T(2,128)S(1)} collective-permute-done((f32[2,1024]{1,0:T(2,128)S(1)}, f32[2,1024]{1,0:T(2,128)S(1)}, u32[]{:S(2)}, u32[]{:S(2)}) %collective-permute-start.6) | collective-permute-done | bytes 8224 | tf_op jit(solution)/shard_map/ppermute | solution.py:189
  86.2 0.0 copy-start
  86.2 8.6 %output_stage.1 = (bf16[32,1024]{1,0:T(8,128)(2,1)S(1)}, f32[1,1024]{1,0:T(1,128)}, f32[1,1024]{1,0:T(1,128)}) custom-call(bf16[6272,256]{1,0:T(8,128)(2,1)S(1)} %get-tuple-element.48.second_ref, bf16[6272,1024]{1,0:T(8,128)(2,1)} %bitcast.11, f32[2,1024]{1,0:T(2,128)S(1)} %add.37.sums_ref, f32[1,1024]{1,0:T(1,128)S(1)} %slice.33.gain_ref, ...), custom_call_target="tpu_custom_call" | custom-call | flops 3288334336 | bytes 6422528 | tf_op jit(solution)/shard_map/output_stage/pallas_call | solution.py:476
  94.8 0.0 collective-permute-done.7.other_ref
  94.8 0.0 copy-done
  94.8 1.2 %probe_stage.1 = f32[1,128]{1,0:T(1,128)S(1)} custom-call(s32[2]{0:T(128)S(1)} %pad_add_fusion.own_ref, s32[32]{0:T(128)S(1)} %copy-done, bf16[32,1024]{1,0:T(8,128)(2,1)S(1)} %get-tuple-element.52.pooled_ref, bf16[32,128,128]{2,1,0:T(8,128)(2,1)S(1)} %slice.28.mine_ref, bf16[32,128,128]{2,1,0:T(8,128)(2,1)S(1)} %collective-permute-done.7.other_ref, ...), custom_call_target="tpu_custom_call" | custom-call | tf_op jit(solution)/shard_map/probe_stage/pallas_call | solution.py:533
  96.0 0.1 collective-permute-start.8
  96.1 1.1 collective-permute-done.8
  97.2 1.0 collective-permute-start.9
  98.2 2.5 %collective-permute-done.9 = f32[1,128]{1,0:T(1,128)S(1)} collective-permute-done((f32[1,128]{1,0:T(1,128)S(1)}, f32[1,128]{1,0:T(1,128)S(1)}, u32[]{:S(2)}, u32[]{:S(2)}) %collective-permute-start.9) | collective-permute-done | bytes 544 | tf_op jit(solution)/shard_map/ppermute | solution.py:189
  100.8 15.2 %all_to_all.15 = f32[32,1,128]{2,1,0:T(1,128)S(1)} all-to-all(f32[32,1,128]{2,1,0:T(1,128)S(1)} %broadcast_in_dim.9), channel_id=1, replica_groups=mesh['pz'=2,'px'=4,'py'=4,'bz'=2,'core'=2] {'pz','px','py'}, dimensions={0} | all-to-all | bytes 32768 | tf_op jit(solution)/shard_map/all_to_all | solution.py:184
  116.0 0.8 slice_reduce_fusion
  (12 shorter events, 0.1 us)
Async XLA Ops:
  3.5 23.9 %all-to-all-start = ((bf16[32,32,256]{2,1,0:T(8,128)(2,1)}), bf16[32,32,256]{2,1,0:T(8,128)(2,1)S(1)}, u32[]{:S(2)}, u32[]{:S(2)}) async-start(bf16[32,32,256]{2,1,0:T(8,128)(2,1)} %get-tuple-element.31), calls=%async_computation | async-start | bytes 1048576 | tf_op jit(solution)/shard_map/all_to_all | solution.py:184
  27.4 29.7 %all-to-all-start.1 = ((bf16[32,232,128]{2,1,0:T(8,128)(2,1)}), bf16[32,232,128]{2,1,0:T(8,128)(2,1)S(1)}, u32[]{:S(2)}, u32[]{:S(2)}) async-start(bf16[32,232,128]{2,1,0:T(8,128)(2,1)} %other_weights.1), calls=%async_computation.1 | async-start | bytes 3801088 | tf_op jit(solution)/shard_map/all_to_all | solution.py:184
  39.5 1.2 %collective-permute-start = (f32[2,256]{1,0:T(2,128)S(1)}, f32[2,256]{1,0:T(2,128)S(1)}, u32[]{:S(2)}, u32[]{:S(2)}) collective-permute-start(f32[2,256]{1,0:T(2,128)S(1)} %get-tuple-element.35), channel_id=1, source_target_pairs={{0,1},{1,0},{2,3},{3,2},{4,5},{5,4},{6,7},{7,6},{8,9},{9,8},{10,11... | collective-permute-start | bytes 6152 | tf_op jit(solution)/shard_map/ppermute | solution.py:188
  40.7 3.7 %collective-permute-start.1 = (f32[2,256]{1,0:T(2,128)S(1)}, f32[2,256]{1,0:T(2,128)S(1)}, u32[]{:S(2)}, u32[]{:S(2)}) collective-permute-start(f32[2,256]{1,0:T(2,128)S(1)} %add.32), channel_id=1, source_target_pairs={{0,2},{2,0},{1,3},{3,1},{4,6},{6,4},{5,7},{7,5},{8,10},{10,8},{9,1... | collective-permute-start | bytes 6152 | tf_op jit(solution)/shard_map/ppermute | solution.py:189
  57.1 2.5 %collective-permute-start.2 = (bf16[32,104,128]{2,1,0:T(8,128)(2,1)S(1)}, bf16[32,104,128]{2,1,0:T(8,128)(2,1)S(1)}, u32[]{:S(2)}, u32[]{:S(2)}) collective-permute-start(bf16[32,104,128]{2,1,0:T(8,128)(2,1)S(1)} %slice.27.mine_ref), channel_id=1, source_target_pairs={{0,1},{1,0},{2,3},{3,2},{4,5},{5,4},{6,7},{7,6},{8,9},{9,8},{10,11... | collective-permute-start | bytes 2555912 | tf_op jit(solution)/shard_map/ppermute | solution.py:570
  59.6 35.2 %collective-permute-start.7 = (bf16[32,128,128]{2,1,0:T(8,128)(2,1)S(1)}, bf16[32,128,128]{2,1,0:T(8,128)(2,1)S(1)}, u32[]{:S(2)}, u32[]{:S(2)}) collective-permute-start(bf16[32,128,128]{2,1,0:T(8,128)(2,1)S(1)} %slice.28.mine_ref), channel_id=1, source_target_pairs={{0,1},{1,0},{2,3},{3,2},{4,5},{5,4},{6,7},{7,6},{8,9},{9,8},{10,11... | collective-permute-start | bytes 3145736 | tf_op jit(solution)/shard_map/ppermute | solution.py:572
  72.8 1.3 %collective-permute-start.3 = (f32[2,256]{1,0:T(2,128)S(1)}, f32[2,256]{1,0:T(2,128)S(1)}, u32[]{:S(2)}, u32[]{:S(2)}) collective-permute-start(f32[2,256]{1,0:T(2,128)S(1)} %get-tuple-element.44), channel_id=1, source_target_pairs={{0,1},{1,0},{2,3},{3,2},{4,5},{5,4},{6,7},{7,6},{8,9},{9,8},{10,11... | collective-permute-start | bytes 6152 | tf_op jit(solution)/shard_map/ppermute | solution.py:188
  74.1 3.6 %collective-permute-start.4 = (f32[2,256]{1,0:T(2,128)S(1)}, f32[2,256]{1,0:T(2,128)S(1)}, u32[]{:S(2)}, u32[]{:S(2)}) collective-permute-start(f32[2,256]{1,0:T(2,128)S(1)} %add.34), channel_id=1, source_target_pairs={{0,2},{2,0},{1,3},{3,1},{4,6},{6,4},{5,7},{7,5},{8,10},{10,8},{9,1... | collective-permute-start | bytes 6152 | tf_op jit(solution)/shard_map/ppermute | solution.py:189
  81.3 1.3 %collective-permute-start.5 = (f32[2,1024]{1,0:T(2,128)S(1)}, f32[2,1024]{1,0:T(2,128)S(1)}, u32[]{:S(2)}, u32[]{:S(2)}) collective-permute-start(f32[2,1024]{1,0:T(2,128)S(1)} %get-tuple-element.49), channel_id=1, source_target_pairs={{0,1},{1,0},{2,3},{3,2},{4,5},{5,4},{6,7},{7,6},{8,9},{9,8},{10,11... | collective-permute-start | bytes 24584 | tf_op jit(solution)/shard_map/ppermute | solution.py:188
  82.5 3.7 %collective-permute-start.6 = (f32[2,1024]{1,0:T(2,128)S(1)}, f32[2,1024]{1,0:T(2,128)S(1)}, u32[]{:S(2)}, u32[]{:S(2)}) collective-permute-start(f32[2,1024]{1,0:T(2,128)S(1)} %add.36), channel_id=1, source_target_pairs={{0,2},{2,0},{1,3},{3,1},{4,6},{6,4},{5,7},{7,5},{8,10},{10,8},{9,1... | collective-permute-start | bytes 24584 | tf_op jit(solution)/shard_map/ppermute | solution.py:189
  86.2 8.6 %copy-start = (s32[32]{0:T(128)S(1)}, s32[32]{0:T(128)}, u32[]{:S(2)}) copy-start(s32[32]{0:T(128)} %labels_ref.1) | copy-start | bytes 388
  96.0 1.2 %collective-permute-start.8 = (f32[1,128]{1,0:T(1,128)S(1)}, f32[1,128]{1,0:T(1,128)S(1)}, u32[]{:S(2)}, u32[]{:S(2)}) collective-permute-start(f32[1,128]{1,0:T(1,128)S(1)} %probe_stage.1), channel_id=1, source_target_pairs={{0,1},{1,0},{2,3},{3,2},{4,5},{5,4},{6,7},{7,6},{8,9},{9,8},{10,11... | collective-permute-start | bytes 1544 | tf_op jit(solution)/shard_map/ppermute | solution.py:188
  97.2 3.6 %collective-permute-start.9 = (f32[1,128]{1,0:T(1,128)S(1)}, f32[1,128]{1,0:T(1,128)S(1)}, u32[]{:S(2)}, u32[]{:S(2)}) collective-permute-start(f32[1,128]{1,0:T(1,128)S(1)} %add.38), channel_id=1, source_target_pairs={{0,2},{2,0},{1,3},{3,1},{4,6},{6,4},{5,7},{7,5},{8,10},{10,8},{9,1... | collective-permute-start | bytes 1544 | tf_op jit(solution)/shard_map/ppermute | solution.py:189
